TPU v7x, 32 devices: a whole 2x2x4 slice. The times are simulated.
32 devices in a mesh: dp: 4 (over z), mp: 8 (over y, x, core).
Axes of the slice: x: 2, y: 2, z: 4, core: 2. Of those that a mesh axis runs over, the one named last changes fastest.
Arguments:
- tokens: bfloat16 [21376, 1152], P(('dp', 'mp')), may hold values from -6 to 6
- skip_tokens: bfloat16 [21376, 1152], P(('dp', 'mp')), may hold values from -6 to 6
- caption_lengths: int32 [64], P('dp'), may hold values from 1 to 77
- output_cotangent: bfloat16 [21376, 1152], P(('dp', 'mp')), may hold values from -6 to 6
- skip_weight: bfloat16 [2304, 1152], P(('dp', 'mp')), may hold values from -0.125 to 0.125
- norm_gains: bfloat16 [2, 1152], P(None, ('dp', 'mp')), may hold values from 0.099609375 to 1.8984375
- bias_rows: bfloat16 [5, 1152], P(None, ('dp', 'mp')), may hold values from -3 to 3
- input_weight: bfloat16 [1152, 3, 1152], P('dp', None, 'mp'), may hold values from -0.25 to 0.25
- output_weight: bfloat16 [1152, 1152], P('mp', 'dp'), may hold values from -0.5 to 0.5
- up_weight: bfloat16 [1152, 4608], P('dp', 'mp'), may hold values from -0.1875 to 0.1875
- up_bias: bfloat16 [4608], P(('mp', 'dp')), may hold values from -3 to 3
- down_weight: bfloat16 [4608, 1152], P('mp', 'dp'), may hold values from -0.125 to 0.125
Outputs:
- output: bfloat16 [21376, 1152], P(('dp', 'mp'))
- grad_tokens: bfloat16 [21376, 1152], P(('dp', 'mp'))
- grad_skip_tokens: bfloat16 [21376, 1152], P(('dp', 'mp'))
- grad_skip_weight: float32 [2304, 1152], P(('dp', 'mp'))
- grad_norm_gains: float32 [2, 1152], P(None, ('dp', 'mp'))
- grad_bias_rows: float32 [5, 1152], P(None, ('dp', 'mp'))
- grad_input_weight: float32 [1152, 3, 1152], P('dp', None, 'mp')
- grad_output_weight: float32 [1152, 1152], P('mp', 'dp')
- grad_up_weight: float32 [1152, 4608], P('dp', 'mp')
- grad_up_bias: float32 [4608], P(('mp', 'dp'))
- grad_down_weight: float32 [4608, 1152], P('mp', 'dp')
All inputs are finite; a program needn't handle non-finite values.
Results may differ from a plain program's by a relative error of at most 0.023.
Values may be sent and summed in bfloat16 or wider, within the bound.
A program may use at most 256 MiB of HBM per device.

v0:
```python
import jax
import jax.numpy as jnp
from jax import lax
from jax.sharding import PartitionSpec as P

HD = 72
CAP = 77
ITEMS_DEV = 16
SEQ = 334


norm_eps = 1e-05
masked_score = -1e30


def layer_norm(values, weight, offset):
    average = jnp.mean(values, -1, keepdims=True)
    centred = values - average
    spread = jnp.mean(centred * centred, -1, keepdims=True)
    return centred * lax.rsqrt(spread + norm_eps) * weight + offset


def exact_gelu(values):
    return jax.nn.gelu(values, approximate=False)


def group_size(item_count, length):
    for option in range(1, item_count + 1):
        if item_count % option == 0 and option * length >= 512:
            return option
    return item_count


def score_block(query_rows, key_rows, valid_rows):
    scores = jnp.einsum(
        "bqhd,bkhd->bhqk", query_rows, key_rows, preferred_element_type=jnp.float32
    ) * HD ** (-0.5)
    return jnp.where(valid_rows[:, None, None, :], scores, masked_score)


def attend_forward(packed):
    query_rows, key_rows, value_rows, valid_rows = packed
    scores = score_block(query_rows, key_rows, valid_rows)
    highest = jnp.max(scores, -1, keepdims=True)
    expanded = jnp.exp(scores - highest)
    row_sums = jnp.sum(expanded, -1, keepdims=True)
    prob_rows = (expanded / row_sums).astype(jnp.bfloat16)
    mixed_rows = jnp.einsum(
        "bhqk,bkhd->bqhd", prob_rows, value_rows, preferred_element_type=jnp.float32
    )
    log_total = highest[..., 0] + jnp.log(row_sums[..., 0])
    return (mixed_rows.astype(jnp.bfloat16), log_total)


def attend_backward(packed):
    query_rows, key_rows, value_rows, valid_rows, grad_mixed, log_total = packed
    scores = score_block(query_rows, key_rows, valid_rows)
    prob_rows = jnp.exp(scores - log_total[..., None])
    rounded = prob_rows.astype(jnp.bfloat16)
    grad_values = jnp.einsum(
        "bhqk,bqhd->bkhd", rounded, grad_mixed, preferred_element_type=jnp.float32
    )
    grad_probs = jnp.einsum(
        "bqhd,bkhd->bhqk", grad_mixed, value_rows, preferred_element_type=jnp.float32
    )
    inner_sum = jnp.sum(prob_rows * grad_probs, -1, keepdims=True)
    grad_scores = (prob_rows * (grad_probs - inner_sum)).astype(jnp.bfloat16)
    scale_factor = HD ** (-0.5)
    grad_query = (
        jnp.einsum("bhqk,bkhd->bqhd", grad_scores, key_rows, preferred_element_type=jnp.float32)
        * scale_factor
    )
    grad_keys = (
        jnp.einsum("bhqk,bqhd->bkhd", grad_scores, query_rows, preferred_element_type=jnp.float32)
        * scale_factor
    )
    return jnp.stack([grad_query, grad_keys, grad_values], axis=2).astype(jnp.bfloat16)


def shards(
    tokens,
    skip_tokens,
    caption_lengths,
    output_cotangent,
    skip_weight,
    norm_gains,
    bias_rows,
    input_weight,
    output_weight,
    up_weight,
    up_bias,
    down_weight,
):
    full_skip, gain_rows, shift_rows = (
        lax.all_gather(skip_weight, ("dp", "mp"), axis=0, tiled=True),
        lax.all_gather(norm_gains, ("dp", "mp"), axis=1, tiled=True),
        lax.all_gather(bias_rows, ("dp", "mp"), axis=1, tiled=True),
    )
    gain_rows = gain_rows.astype(jnp.float32)
    shift_rows = shift_rows.astype(jnp.float32)
    in_full, out_full, up_full, down_full, up_shift = (
        lax.all_gather(input_weight, "dp", axis=0, tiled=True),
        lax.all_gather(output_weight, "dp", axis=1, tiled=True),
        lax.all_gather(up_weight, "dp", axis=0, tiled=True),
        lax.all_gather(down_weight, "dp", axis=1, tiled=True),
        lax.all_gather(up_bias, "dp", axis=0, tiled=True),
    )
    local_rows = tokens.shape[0]
    feature_total = tokens.shape[1]
    group_rows = local_rows * lax.axis_size("mp")
    positions = jnp.arange(SEQ, dtype=jnp.int32)
    joined = jnp.concatenate([tokens, skip_tokens], axis=1)
    hidden = jnp.dot(joined, full_skip, preferred_element_type=jnp.float32) + shift_rows[0]
    normed = layer_norm(hidden, gain_rows[0], shift_rows[1]).astype(jnp.bfloat16)
    head_width = in_full.shape[2]
    head_count = head_width // HD
    in_flat = in_full.reshape(in_full.shape[0], 3 * head_width)
    group_items = group_size(ITEMS_DEV, SEQ)
    group_count = ITEMS_DEV // group_items
    key_valid = (
        (positions[None, :] < 1)
        | (positions[None, :] > CAP)
        | (positions[None, :] - 1 < caption_lengths[:, None])
    )
    normed_rows = lax.all_gather(normed, "mp", axis=0, tiled=True)
    triples = jnp.dot(normed_rows, in_flat, preferred_element_type=jnp.float32).astype(jnp.bfloat16)
    shaped = triples.reshape(group_count, group_items, SEQ, 3, head_count, HD)
    valid_all = key_valid.reshape(group_count, group_items, SEQ)
    query_all = shaped[:, :, :, 0]
    key_all = shaped[:, :, :, 1]
    value_all = shaped[:, :, :, 2]
    mixed_all, log_totals = lax.map(attend_forward, (query_all, key_all, value_all, valid_all))
    mixed_rows = mixed_all.reshape(group_rows, head_width)
    piece = mixed_rows
    attention = lax.psum_scatter(
        jnp.dot(piece, out_full, preferred_element_type=jnp.float32).astype(jnp.bfloat16),
        "mp",
        scatter_dimension=0,
        tiled=True,
    ).astype(jnp.float32)
    middle = hidden + attention + shift_rows[2]
    normed_two = layer_norm(middle, gain_rows[1], shift_rows[3]).astype(jnp.bfloat16)
    grad_output = output_cotangent.astype(jnp.float32)
    up_whole, down_whole, shift_whole = (
        lax.all_gather(up_full, "mp", axis=1, tiled=True),
        lax.all_gather(down_full, "mp", axis=0, tiled=True),
        lax.all_gather(up_shift, "mp", axis=0, tiled=True),
    )
    before = jnp.dot(normed_two, up_whole, preferred_element_type=jnp.float32) + shift_whole.astype(
        jnp.float32
    )
    active = exact_gelu(before).astype(jnp.bfloat16)
    branch = jnp.dot(active, down_whole, preferred_element_type=jnp.float32)
    grad_active = jnp.dot(output_cotangent, down_whole.T, preferred_element_type=jnp.float32)
    grad_down_whole = jnp.dot(active.T, output_cotangent, preferred_element_type=jnp.float32)
    grad_before = jax.vjp(exact_gelu, before)[1](grad_active)[0].astype(jnp.bfloat16)
    grad_up_whole = jnp.dot(normed_two.T, grad_before, preferred_element_type=jnp.float32)
    grad_shift_whole = jnp.sum(grad_before.astype(jnp.float32), 0)
    grad_normed_two = jnp.dot(grad_before, up_whole.T, preferred_element_type=jnp.float32)
    grad_up, grad_down, grad_up_shift = (
        lax.psum_scatter(
            grad_up_whole.astype(jnp.bfloat16), "mp", scatter_dimension=1, tiled=True
        ).astype(jnp.float32),
        lax.psum_scatter(
            grad_down_whole.astype(jnp.bfloat16), "mp", scatter_dimension=0, tiled=True
        ).astype(jnp.float32),
        lax.psum_scatter(
            grad_shift_whole.astype(jnp.bfloat16), "mp", scatter_dimension=0, tiled=True
        ).astype(jnp.float32),
    )
    output = (middle + branch + shift_rows[4]).astype(jnp.bfloat16)
    second_pull = jax.vjp(layer_norm, middle, gain_rows[1], shift_rows[3])[1]
    grad_middle_part, grad_gain_two, grad_shift_three = second_pull(grad_normed_two)
    grad_middle = grad_output + grad_middle_part
    grad_attention = grad_middle.astype(jnp.bfloat16)
    attention_rows = lax.all_gather(grad_attention, "mp", axis=0, tiled=True)
    grad_mixed = jnp.dot(attention_rows, out_full.T, preferred_element_type=jnp.float32).astype(
        jnp.bfloat16
    )
    grad_out_weight = jnp.dot(mixed_rows.T, attention_rows, preferred_element_type=jnp.float32)
    grad_mixed_all = grad_mixed.reshape(group_count, group_items, SEQ, head_count, HD)
    grads_all = lax.map(
        attend_backward, (query_all, key_all, value_all, valid_all, grad_mixed_all, log_totals)
    )
    grad_triples = grads_all.reshape(group_rows, 3 * head_width)
    grad_in_weight = jnp.dot(
        normed_rows.T, grad_triples, preferred_element_type=jnp.float32
    ).reshape(in_full.shape)
    piece = grad_triples
    grad_normed = lax.psum_scatter(
        jnp.dot(piece, in_flat.T, preferred_element_type=jnp.float32).astype(jnp.bfloat16),
        "mp",
        scatter_dimension=0,
        tiled=True,
    ).astype(jnp.float32)
    first_pull = jax.vjp(layer_norm, hidden, gain_rows[0], shift_rows[1])[1]
    grad_hidden_part, grad_gain_one, grad_shift_one = first_pull(grad_normed)
    grad_hidden = (grad_middle + grad_hidden_part).astype(jnp.bfloat16)
    grad_joined = jnp.dot(grad_hidden, full_skip.T, preferred_element_type=jnp.float32).astype(
        jnp.bfloat16
    )
    grad_token_rows = grad_joined[:, :feature_total]
    grad_skip_rows = grad_joined[:, feature_total:]
    grad_skip_weight = jnp.dot(joined.T, grad_hidden, preferred_element_type=jnp.float32)
    grad_gains = jnp.stack([grad_gain_one, grad_gain_two])
    grad_shifts = jnp.stack(
        [
            jnp.sum(grad_hidden.astype(jnp.float32), 0),
            grad_shift_one,
            jnp.sum(grad_attention.astype(jnp.float32), 0),
            grad_shift_three,
            jnp.sum(grad_output, 0),
        ]
    )
    skip_grads, gain_grads, shift_grads = (
        lax.psum_scatter(grad_skip_weight, ("dp", "mp"), scatter_dimension=0, tiled=True),
        lax.psum_scatter(grad_gains, ("dp", "mp"), scatter_dimension=1, tiled=True),
        lax.psum_scatter(grad_shifts, ("dp", "mp"), scatter_dimension=1, tiled=True),
    )
    in_grads, out_grads, up_grads, down_grads, up_shift_grads = (
        lax.psum_scatter(
            grad_in_weight.astype(jnp.bfloat16), "dp", scatter_dimension=0, tiled=True
        ).astype(jnp.float32),
        lax.psum_scatter(
            grad_out_weight.astype(jnp.bfloat16), "dp", scatter_dimension=1, tiled=True
        ).astype(jnp.float32),
        lax.psum_scatter(
            grad_up.astype(jnp.bfloat16), "dp", scatter_dimension=0, tiled=True
        ).astype(jnp.float32),
        lax.psum_scatter(
            grad_down.astype(jnp.bfloat16), "dp", scatter_dimension=1, tiled=True
        ).astype(jnp.float32),
        lax.psum_scatter(
            grad_up_shift.astype(jnp.bfloat16), "dp", scatter_dimension=0, tiled=True
        ).astype(jnp.float32),
    )
    return (
        output,
        grad_token_rows,
        grad_skip_rows,
        skip_grads,
        gain_grads,
        shift_grads,
        in_grads,
        out_grads,
        up_grads,
        up_shift_grads,
        down_grads,
    )


def solution(mesh):
    in_specs = (
        P(("dp", "mp"), None),
        P(("dp", "mp"), None),
        P("dp"),
        P(("dp", "mp"), None),
        P(("dp", "mp"), None),
        P(None, ("dp", "mp")),
        P(None, ("dp", "mp")),
        P("dp", None, "mp"),
        P("mp", "dp"),
        P("dp", "mp"),
        P(("mp", "dp")),
        P("mp", "dp"),
    )
    out_specs = (
        P(("dp", "mp"), None),
        P(("dp", "mp"), None),
        P(("dp", "mp"), None),
        P(("dp", "mp"), None),
        P(None, ("dp", "mp")),
        P(None, ("dp", "mp")),
        P("dp", None, "mp"),
        P("mp", "dp"),
        P("dp", "mp"),
        P(("mp", "dp")),
        P("mp", "dp"),
    )
    return jax.shard_map(shards, mesh=mesh, in_specs=in_specs, out_specs=out_specs, check_vma=False)
```

profile of v0, /device:TPU:0, one launch (start us, length us, event | category | flops | bytes accessed | tf_op | source)
XLA Modules:
  0.0 1327.9 jit_solution(511702719467062029)
XLA Ops:
  9.5 44.0 %all-gather = bf16[32,36,5]{1,2,0:T(8,128)(2,1)S(1)} all-gather(bf16[1,36,5]{1,2,0:T(8,128)(2,1)} %bitcast.201), channel_id=1, replica_groups=mesh['dp'=4,'mp'=8] {'dp','mp'}, dimensions={0}, use_global_device_ids=true | all-gather | bytes 11880 | tf_op jit(solution)/shard_map/all_gather | solution.py:97
  56.9 36.9 %all-gather.1 = bf16[32,36,2]{1,2,0:T(2,128)(2,1)S(1)} all-gather(bf16[1,36,2]{1,2,0:T(2,128)(2,1)S(1)} %bitcast.202), channel_id=1, replica_groups=mesh['dp'=4,'mp'=8] {'dp','mp'}, dimensions={0}, use_global_device_ids=true | all-gather | bytes 4752 | tf_op jit(solution)/shard_map/all_gather | solution.py:96
  95.3 7.8 fusion.65
  106.8 8.1 all-gather.15.cloned.1.call-done
  118.7 69.1 %all_gather.43 = bf16[1152,3,144]{2,1,0:T(4,128)(2,1)} all-gather(bf16[288,3,144]{2,1,0:T(4,128)(2,1)} %copy.110), channel_id=1, replica_groups=mesh['dp'=4,'mp'=8] {'dp'}, dimensions={0}, use_global_device_ids=true | all-gather | bytes 1244160 | tf_op jit(solution)/shard_map/all_gather | solution.py:102
  187.9 4.7 copy.111
  193.2 14.5 %all-gather.3 = bf16[4,288,144]{1,2,0:T(8,128)(2,1)S(1)} all-gather(bf16[1,288,144]{1,2,0:T(8,128)(2,1)S(1)} %bitcast.198), channel_id=1, replica_groups=mesh['dp'=4,'mp'=8] {'dp'}, dimensions={0}, use_global_device_ids=true | all-gather | bytes 414720 | tf_op jit(solution)/shard_map/all_gather | solution.py:103
  210.3 2.9 copy.118
  213.5 33.6 %all-gather.23.cloned.1.call-done = bf16[8,668,1152]{2,1,0:T(8,128)(2,1)} async-done(((bf16[1,668,1152]{2,1,0:T(8,128)(2,1)}), bf16[8,668,1152]{2,1,0:T(8,128)(2,1)}) %all-gather.23.cloned.1.call-update) | async-done | bytes 12312592 | tf_op jit(solution)/shard_map/all_gather | solution.py:125
  247.2 10.0 reshape.234
  257.2 15.0 %convolution_convert_fusion.6 = bf16[5344,432]{0,1:T(8,128)(2,1)} fusion(bf16[5344,1152]{1,0:T(8,128)(2,1)} %reshape.234, bf16[1152,432]{0,1:T(8,128)(2,1)} %bitcast.193), kind=kOutput, calls=%fused_computation.75 | convolution fusion | flops 5321341440 | bytes 17925120 | tf_op jit(solution)/shard_map/dot_general | solution.py:126
  272.2 11.6 reshape.215
  283.9 5.5 fusion.61
  293.5 49.1 %while.22 = (s32[]{:T(128)}, bf16[8,2,334,2,72]{2,1,0,4,3:T(2,128)(2,1)}, f32[8,2,2,334]{3,2,1,0:T(2,128)}, bf16[8,2,334,2,72]{2,4,3,1,0:T(8,128)(2,1)}, pred[8,...) while((s32[]{:T(128)}, ...), condition=%wide.region_5.6_spmd, body=%wide.region_2.5_spmd.sunk | while | flops 133962056 | bytes 6672217 | solution.py:132
  342.5 4.5 reshape.216
  347.0 9.8 convolution_convert_fusion.3
  356.8 138.0 %fusion = bf16[672,1152]{1,0:T(8,128)(2,1)} fusion(bf16[5344,1152]{1,0:T(8,128)(2,1)} %convolution_convert_fusion.3), kind=kCustom, calls=%all-reduce-scatter | all-reduce-scatter fusion | flops 6193153 | bytes 13861376
  499.3 11.7 all-reduce
  511.2 22.8 %all-reduce.1 = bf16[4608]{0:T(1024)(128)(2,1)S(1)} all-reduce(bf16[4608]{0:T(1024)(128)(2,1)S(1)} %dynamic-update-slice.1), channel_id=1, replica_groups=mesh['dp'=4,'mp'=8] {'mp'}, use_global_device_ids=true, to_apply=%add.1 | all-reduce | flops 4608 | bytes 18432
  534.6 9.8 concatenate.12
  549.2 14.9 %fusion.55 = f32[668,4608]{1,0:T(8,128)} fusion(bf16[1152,4608]{0,1:T(8,128)(2,1)} %all-gather.17.cloned.1.call-done, f32[668,1152]{1,0:T(8,128)} %copy-done.2, f32[1152]{0:T(1024)S(1)} %copy-done.35, f32[1152]{0:T(1024)S(1)} %get-tuple-element.219, f32[668]{0:T(1024)S(1)} %fusion.52, f32[668]{0:T(1024)S(1)} %broadcast_multiply_fusion), kind=kOutput, calls=%fused_computation.141 | convolution fusion | flops 7095891456 | bytes 26022112 | tf_op jit(solution)/shard_map/dot_general | solution.py:149
  564.1 41.2 %fusion.56 = (bf16[4608]{0:T(1024)(128)(2,1)}, bf16[668,4608]{1,0:T(8,128)(2,1)S(1)}, f32[668,4608]{1,0:T(8,128)}) fusion(f32[668,4608]{1,0:T(8,128)} %fusion.55, f32[4608]{0:T(1024)S(1)} %convert_element_type.125, bf16[668,1152]{1,0:T(8,128)(2,1)} %param.19, bf16[4608,1152]{1,0:T(8,128)(2,1)} %all-gather.21.cloned.1.call-done), kind=kOutput, calls=%fused_computation.142 | convolution fusion | flops 7319821824 | bytes 42964992 | tf_op jit(solution)/shard_map/dot_general | solution.py:154
  607.9 12.6 convolution_convert_fusion.5
  620.6 12.9 multiply_convert_fusion.1
  633.4 2.8 copy-done.10
  636.2 11.7 convolution_convert_fusion.4
  648.0 16.4 %multiply_reduce_fusion.1 = (f32[1152]{0:T(1024)S(1)}, f32[668]{0:T(1024)S(1)}, f32[1152]{0:T(1024)S(1)}, f32[668,1152]{1,0:T(8,128)S(1)}) fusion(f32[668,1152]{1,0:T(8,128)S(1)} %copy-done.3, f32[668]{0:T(1024)S(1)} %fusion.52, f32[668]{0:T(1024)S(1)} %broadcast_multiply_fusion, f32[1152]{0:T(1024)S(1)} %get-tuple-element.219, ...), kind=kOutput, calls=%fused_computation.95 | convolution fusion | flops 7098197504 | bytes 22951248 | tf_op jit(solution)/shard_map/dot_general | solution.py:159
  667.5 33.2 %reduce-scatter.24.cloned.1.call-done = bf16[1152,576]{0,1:T(8,128)(2,1)} async-done(((bf16[1152,4608]{0,1:T(8,128)(2,1)}), bf16[1152,576]{0,1:T(8,128)(2,1)}) %reduce-scatter.24.cloned.1.call-update) | async-done | bytes 1327120 | tf_op jit(solution)/shard_map/reduce_scatter | solution.py:161
  703.5 11.1 reshape.245
  714.5 72.4 %reduce-scatter.26.cloned.1.call-done = bf16[576,1152]{1,0:T(8,128)(2,1)} async-done(((bf16[4608,1152]{1,0:T(8,128)(2,1)}), bf16[576,1152]{1,0:T(8,128)(2,1)}) %reduce-scatter.26.cloned.1.call-update) | async-done | bytes 1327120 | tf_op jit(solution)/shard_map/reduce_scatter | solution.py:164
  789.6 71.0 %all-gather.25.cloned.1.call-done = bf16[8,668,1152]{2,1,0:T(8,128)(2,1)} async-done(((bf16[1,668,1152]{2,1,0:T(8,128)(2,1)}), bf16[8,668,1152]{2,1,0:T(8,128)(2,1)}) %all-gather.25.cloned.1.call-update) | async-done | bytes 12312592 | tf_op jit(solution)/shard_map/all_gather | solution.py:176
  860.6 9.8 reshape.238
  870.5 8.0 convolution_convert_fusion.7
  878.4 3.0 reshape.217
  881.4 79.2 %while.23 = (s32[]{:T(128)}, bf16[8,2,334,3,2,72]{2,1,0,5,4,3:T(2,128)(2,1)}, bf16[8,2,334,2,72]{2,4,3,1,0:T(8,128)(2,1)}, pred[8,2,334]{2,1,0:T(4,128)(4,1)}, b...) while((s32[]{:T(128)}, ...), condition=%wide.region_13.14_spmd, body=%wide.region_11.13_spmd.sunk | while | flops 326354048 | bytes 18264212 | solution.py:182
  960.7 9.7 reshape.218
  970.4 13.6 %convolution_convert_fusion.2 = bf16[5344,1152]{1,0:T(8,128)(2,1)} fusion(bf16[5344,432]{0,1:T(8,128)(2,1)} %reshape.218, bf16[1152,432]{0,1:T(8,128)(2,1)S(1)} %bitcast.194), kind=kOutput, calls=%fused_computation.54 | convolution fusion | flops 5325189120 | bytes 17925120 | tf_op jit(solution)/shard_map/dot_general | solution.py:191
  984.0 124.8 %fusion.1 = bf16[672,1152]{1,0:T(8,128)(2,1)S(1)} fusion(bf16[5344,1152]{1,0:T(8,128)(2,1)} %convolution_convert_fusion.2), kind=kCustom, calls=%all-reduce-scatter.1 | all-reduce-scatter fusion | flops 6193153 | bytes 13861376
  1110.8 6.7 convolution_convert_fusion.10
  1118.7 12.4 convolution_convert_fusion.9
  1133.7 9.8 concatenate.13
  1151.8 7.4 fusion.66
  1160.9 23.3 %all-reduce.7 = bf16[4608]{0:T(1024)(128)(2,1)S(1)} all-reduce(bf16[4608]{0:T(1024)(128)(2,1)S(1)} %copy-done.33), channel_id=11, replica_groups=mesh['dp'=4,'mp'=8] {'mp'}, use_global_device_ids=true, to_apply=%region_32.33.clone | all-reduce | flops 4608 | bytes 18432
  1184.3 11.4 all-reduce.8
  1196.4 14.9 %fusion.46 = bf16[668,1152]{1,0:T(8,128)(2,1)} fusion(f32[668,1152]{1,0:T(8,128)S(1)} %copy-done.4, bf16[668,4608]{1,0:T(8,128)(2,1)} %copy-done.10, bf16[4608,1152]{1,0:T(8,128)(2,1)} %all-gather.21.cloned.1.call-done, f32[1152]{0:T(1024)S(1)} %copy-done.34), kind=kOutput, calls=%fused_computation.90 | convolution fusion | flops 7094352384 | bytes 21394944 | tf_op jit(solution)/shard_map/dot_general | solution.py:153
  1216.2 42.9 %all-reduce.11 = (f32[2,1152]{1,0:T(2,128)S(1)}, f32[5,1152]{1,0:T(8,128)S(1)}) all-reduce(f32[2,1152]{1,0:T(2,128)S(1)} %pad_maximum_fusion.1, f32[5,1152]{1,0:T(8,128)S(1)} %stack.35), channel_id=5, replica_groups=mesh['dp'=4,'mp'=8] {'dp','mp'}, use_global_device_ids=true, to_apply=%region_20.21.clone | all-reduce | flops 8064 | bytes 64512
  1260.4 7.1 convolution_convert_fusion.8
  1273.2 47.9 %reduce-scatter.36.cloned.1.call-done = f32[72,1152]{1,0:T(8,128)} async-done(((f32[2304,1152]{1,0:T(8,128)}), f32[72,1152]{1,0:T(8,128)}) %reduce-scatter.36.cloned.1.call-update) | async-done | bytes 331792
  (331 shorter events, 195.9 us)
Async XLA Ops:
  7.2 49.7 %copy-start.38 = (bf16[2,36]{1,0:T(2,128)(2,1)S(1)}, bf16[2,36]{1,0:T(2,128)(2,1)}, u32[]{:S(2)}) copy-start(bf16[2,36]{1,0:T(2,128)(2,1)} %param.21) | copy-start | bytes 436
  7.2 86.8 %copy-start.16 = (bf16[668,1152]{1,0:T(8,128)(2,1)S(1)}, bf16[668,1152]{1,0:T(8,128)(2,1)}, u32[]{:S(2)}) copy-start(bf16[668,1152]{1,0:T(8,128)(2,1)} %param.17) | copy-start | bytes 4617220
  7.2 88.1 %all-gather.13.cloned.1.call-start = ((), (), s32[]{:S(2)}) async-start(), calls=%async_computation.7 | async-start | bytes 5474304 | tf_op jit(solution)/shard_map/all_gather | solution.py:95
  7.9 107.0 %all-gather.15.cloned.1.call-start = ((), (), s32[]{:S(2)}) async-start(), calls=%async_computation.8 | async-start | bytes 1843200 | tf_op jit(solution)/shard_map/all_gather | solution.py:104
  8.7 201.7 %all-gather.19.cloned.1.call-start = ((), (), s32[]{:S(2)}) async-start(), calls=%async_computation.10 | async-start | bytes 1843200 | tf_op jit(solution)/shard_map/all_gather | solution.py:105
  9.4 237.7 %all-gather.23.cloned.1.call-start = ((), (), s32[]{:S(2)}) async-start(), calls=%async_computation.14 | async-start | bytes 13934592 | tf_op jit(solution)/shard_map/all_gather | solution.py:125
  94.0 10.5 copy-start.22
  103.1 441.3 %copy-start = (f32[668,1152]{1,0:T(8,128)}, f32[668,1152]{1,0:T(8,128)S(1)}, u32[]{:S(2)}) copy-start(f32[668,1152]{1,0:T(8,128)S(1)} %get-tuple-element.280) | copy-start | bytes 9234436
  106.7 10.8 copy-start.21
  106.8 442.4 %all-gather.17.cloned.1.call-start = ((), (), s32[]{:S(2)}) async-start(), calls=%async_computation.9 | async-start | bytes 11943936 | tf_op jit(solution)/shard_map/all_gather | solution.py:145
  117.5 446.6 %all-gather.21.cloned.1.call-start = ((), (), s32[]{:S(2)}) async-start(), calls=%async_computation.11 | async-start | bytes 11943936 | tf_op jit(solution)/shard_map/all_gather | solution.py:146
  118.7 73.8 %copy-start.39 = (s32[16]{0:T(128)S(1)}, s32[16]{0:T(128)}, u32[]{:S(2)}) copy-start(s32[16]{0:T(128)} %param.18) | copy-start | bytes 196
  118.7 74.5 %copy-start.26 = (bf16[144,288]{1,0:T(8,128)(2,1)S(1)}, bf16[144,288]{1,0:T(8,128)(2,1)}, u32[]{:S(2)}) copy-start(bf16[144,288]{1,0:T(8,128)(2,1)} %param.24) | copy-start | bytes 248836
  213.3 487.5 %reduce-scatter.24.cloned.1.call-start = ((), (), s32[]{:S(2)}) async-start(), calls=%async_computation.12 | async-start | bytes 11943936 | tf_op jit(solution)/shard_map/reduce_scatter | solution.py:161
  342.5 4.5 copy-start.17
  356.8 140.3 %copy-start.36 = (u32[32]{0:T(128)S(1)}, u32[32]{0:T(128)}, u32[]{:S(2)}) copy-start(u32[32]{0:T(128)} %constant.148) | copy-start | bytes 388
  356.8 140.3 %copy-start.37 = (u32[32]{0:T(128)S(1)}, u32[32]{0:T(128)}, u32[]{:S(2)}) copy-start(u32[32]{0:T(128)} %constant.143) | copy-start | bytes 388
  356.8 142.3 %copy-start.40 = (bf16[144]{0:T(256)(128)(2,1)S(1)}, bf16[144]{0:T(256)(128)(2,1)}, u32[]{:S(2)}) copy-start(bf16[144]{0:T(256)(128)(2,1)} %param.26) | copy-start | bytes 868
  495.7 38.9 %collective-permute-start = (bf16[28,1152]{1,0:T(8,128)(2,1)S(1)}, bf16[28,1152]{1,0:T(8,128)(2,1)S(1)}, u32[]{:S(2)}, u32[]{:S(2)}) collective-permute-start(bf16[28,1152]{1,0:T(8,128)(2,1)S(1)} %slice.62), channel_id=1, source_target_pairs={{0,1},{1,2},{2,3},{3,4},{4,5},{5,6},{6,7},{8,9},{9,10},{10,11},{11... | collective-permute-start | bytes 193544
  546.6 2.7 copy-start.35
  564.1 43.7 %copy-start.3 = (f32[668,1152]{1,0:T(8,128)S(1)}, f32[668,1152]{1,0:T(8,128)}, u32[]{:S(2)}) copy-start(f32[668,1152]{1,0:T(8,128)} %copy-done.2) | copy-start | bytes 9234436
  605.3 2.6 copy-start.41
  620.5 166.4 %reduce-scatter.26.cloned.1.call-start = ((), (), s32[]{:S(2)}) async-start(), calls=%async_computation.13 | async-start | bytes 11943936 | tf_op jit(solution)/shard_map/reduce_scatter | solution.py:164
  620.5 15.7 %copy-start.11 = (bf16[668,1152]{1,0:T(8,128)(2,1)S(1)}, bf16[668,1152]{1,0:T(8,128)(2,1)}, u32[]{:S(2)}) copy-start(bf16[668,1152]{1,0:T(8,128)(2,1)} %param.19) | copy-start | bytes 4617220
  633.4 2.8 copy-start.10
  647.9 16.4 %copy-start.32 = (f32[668]{0:T(1024)S(1)}, f32[668]{0:T(1024)}, u32[]{:S(2)}) copy-start(f32[668]{0:T(1024)} %copy-done.31) | copy-start | bytes 8020
  647.9 212.7 %all-gather.25.cloned.1.call-start = ((), (), s32[]{:S(2)}) async-start(), calls=%async_computation.15 | async-start | bytes 13934592 | tf_op jit(solution)/shard_map/all_gather | solution.py:176
  667.5 543.8 %reduce-scatter.32.cloned.1.call-start = ((), (), s32[]{:S(2)}) async-start(), calls=%async_computation.18 | async-start | bytes 1843200
  703.4 510.3 %reduce-scatter.34.cloned.1.call-start = ((), (), s32[]{:S(2)}) async-start(), calls=%async_computation.19 | async-start | bytes 1843200
  789.6 80.9 %copy-start.18 = (bf16[1152,144]{0,1:T(8,128)(2,1)S(1)}, bf16[1152,144]{0,1:T(8,128)(2,1)}, u32[]{:S(2)}) copy-start(bf16[1152,144]{0,1:T(8,128)(2,1)} %reshape.236) | copy-start | bytes 995332
  789.6 479.8 %reduce-scatter.30.cloned.1.call-start = ((), (), s32[]{:S(2)}) async-start(), calls=%async_computation.17 | async-start | bytes 737280
  960.7 9.7 copy-start.19
  984.0 126.8 %copy-start.8 = (bf16[5344,144]{0,1:T(8,128)(2,1)S(1)}, bf16[5344,144]{0,1:T(8,128)(2,1)}, u32[]{:S(2)}) copy-start(bf16[5344,144]{0,1:T(8,128)(2,1)} %reshape.216) | copy-start | bytes 4617220
  1108.8 8.7 copy-start.9
  1109.5 24.2 %collective-permute-start.1 = (bf16[28,1152]{1,0:T(8,128)(2,1)}, bf16[28,1152]{1,0:T(8,128)(2,1)S(1)}, u32[]{:S(2)}, u32[]{:S(2)}) collective-permute-start(bf16[28,1152]{1,0:T(8,128)(2,1)} %slice.63), channel_id=1, source_target_pairs={{0,1},{1,2},{2,3},{3,4},{4,5},{5,6},{6,7},{8,9},{9,10},{10,11},{11... | collective-permute-start | bytes 193544
  1118.6 152.5 %reduce-scatter.28.cloned.1.call-start = ((), (), s32[]{:S(2)}) async-start(), calls=%async_computation.16 | async-start | bytes 1474560
  1131.0 12.5 copy-start.1
  1131.0 12.5 copy-start.23
  1131.0 12.5 copy-start.25
  1133.6 187.5 %reduce-scatter.36.cloned.1.call-start = ((), (), s32[]{:S(2)}) async-start(), calls=%async_computation.20 | async-start | bytes 10948608
  1143.5 2.5 copy-start.30
  1143.6 2.6 copy-start.7
  1143.6 2.6 copy-start.28
  1146.1 2.3 copy-start.13
  1148.4 3.4 copy-start.20
  1159.2 37.2 %copy-start.4 = (f32[668,1152]{1,0:T(8,128)S(1)}, f32[668,1152]{1,0:T(8,128)}, u32[]{:S(2)}) copy-start(f32[668,1152]{1,0:T(8,128)} %copy-done.2) | copy-start | bytes 9234436
  1159.2 37.2 %copy-start.34 = (f32[1152]{0:T(1024)S(1)}, f32[1152]{0:T(1024)}, u32[]{:S(2)}) copy-start(f32[1152]{0:T(1024)} %get-tuple-element.214) | copy-start | bytes 13828
  1211.3 49.1 %copy-start.15 = (bf16[668,1152]{1,0:T(8,128)(2,1)S(1)}, bf16[668,1152]{1,0:T(8,128)(2,1)}, u32[]{:S(2)}) copy-start(bf16[668,1152]{1,0:T(8,128)(2,1)} %copy-done.14) | copy-start | bytes 4617220
  (10 other events, 13.3 us)
Sparse Core Ops, SparseCore 0:
  10.9 68.4 all-gather.12
  81.0 33.8 all-gather.14
  116.5 58.8 all-gather.18
  177.7 69.3 all-gather.22
  249.5 63.6 all-gather.16
  314.9 74.8 all-gather.20
  620.6 80.1 reduce-scatter.23
  704.3 82.5 reduce-scatter.25
  789.4 71.1 all-gather.24
  862.8 33.8 reduce-scatter.31
  899.0 32.7 reduce-scatter.33
  1118.7 23.7 reduce-scatter.29
  1144.9 27.6 reduce-scatter.27
  1179.1 142.0 reduce-scatter.35
where the time goes:
time: 1340 us; the launch traced here: 1330 us
  blocking collectives  540 us (40%)
  matrix products  278 us (21%)
  waiting for transfers between devices  269 us (20%)
  local copies, waits for them, and re-layouts  177 us (13%)
  other arithmetic  42.8 us (3%)
  between operations  18.3 us (1%)
    unnamed x7, blocking collectives  375 us
    unnamed x113, local copies, waits for them, and re-layouts  88.2 us
    reduce_scatter x1, waiting for transfers between devices, shards(): lax.psum_scatter(grad_down_whole.astype(jnp.bfloat16), 'mp', scatter_dime...  72.4 us
    all_gather x1, waiting for transfers between devices, shards(): attention_rows = lax.all_gather(grad_attention, 'mp', axis=0, tiled=True)  71 us
    all_gather x1, blocking collectives, shards(): lax.all_gather(input_weight, 'dp', axis=0, tiled=True)  69.1 us
    unnamed x21, waiting for transfers between devices  50.2 us
    all_gather x1, blocking collectives, shards(): lax.all_gather(bias_rows, ('dp', 'mp'), axis=1, tiled=True)  44 us
    dot_general x1, matrix products, shards(): jnp.dot(output_cotangent, down_whole.T, preferred_element_type=jnp.float32)  41.2 us
  transfers between devices with their start and end apart: 16, of which 6 were waited for; matrix products, arithmetic and copies ran while one was open for 52% of the time, Pallas kernels for 0%

commit v1 on v0

v1 whole, which is shorter than its diff:
```python
import functools

import jax
import jax.numpy as jnp
from jax import lax
from jax.experimental import pallas as pl
from jax.experimental.pallas import tpu as pltpu
from jax.sharding import PartitionSpec as P


HD = 72
CAP = 77
SEQ = 334
EPS = 1e-05
MASKED = -1e30
VMEM_BYTES = 60 * 1024 * 1024


bf16, f32 = jnp.bfloat16, jnp.float32


def dot_nn(a, b):
    return lax.dot_general(a, b, (((1,), (0,)), ((), ())), preferred_element_type=f32)


def dot_nt(a, b):
    return lax.dot_general(a, b, (((1,), (1,)), ((), ())), preferred_element_type=f32)


def dot_tn(a, b):
    return lax.dot_general(a, b, (((0,), (0,)), ((), ())), preferred_element_type=f32)


def tiles_of(extent, tile):
    return extent // tile, extent % tile


def gelu_parts(v):
    a = jnp.abs(v) * 0.7071067811865476
    t = 1.0 / (1.0 + 0.3275911 * a)
    e = jnp.exp(-a * a)
    poly = t * (
        0.254829592
        + t * (-0.284496736 + t * (1.421413741 + t * (-1.453152027 + t * 1.061405429)))
    )
    half = 0.5 * poly * e
    return jnp.where(v < 0, half, 1.0 - half), e * 0.3989422804014327


def ffn_kernel(first, n2, dy, b0, b1, ub, br_in, *rest):
    if first:
        gn_in = None
        br, gn, g0, g1, gub, wu, wd, gu, gd = rest
    else:
        gn_in, br, gn, g0, g1, gub, wu, wd, gu, gd = rest
    h = b0.shape[0] // 2
    wu[:h], wu[h:] = b0[:h], b1[:h]
    wd[:h], wd[h:] = b0[h:], b1[h:]
    br[...] = br_in[...]
    gn[...] = jnp.zeros(gn.shape, f32) if first else gn_in[...]

    def tile(start, size):
        w_up, w_down = wu[pl.ds(start, size), :], wd[pl.ds(start, size), :]
        before = dot_nt(n2[...], w_up) + ub[:, pl.ds(start, size)]
        grad_active = dot_nt(dy[...], w_down)
        cdf, pdf = gelu_parts(before)
        active = (before * cdf).astype(bf16)
        grad_f32 = grad_active * (cdf + before * pdf)
        grad_before = grad_f32.astype(bf16)
        br[...] += dot_nn(active, w_down)
        gn[...] += dot_nn(grad_before, w_up)
        gd[pl.ds(start, size), :] = dot_tn(active, dy[...]).astype(bf16)
        gu[pl.ds(start, size), :] = dot_tn(grad_before, n2[...]).astype(bf16)
        gub[:, pl.ds(start, size)] = jnp.sum(grad_before.astype(f32), 0, keepdims=True)

    size = 256
    count, left = tiles_of(2 * h, size)

    def step(i, carry):
        tile(pl.multiple_of(i * size, size), size)
        return carry

    lax.fori_loop(0, count, step, 0)
    if left:
        tile(count * size, left)
    g0[:h], g1[:h] = gu[:h], gu[h:]
    g0[h:], g1[h:] = gd[:h], gd[h:]


def ffn_pair(n2, dy, b0, b1, ub, br, gn):
    m, d = n2.shape
    h = b0.shape[0] // 2
    block = jax.ShapeDtypeStruct((2 * h, d), bf16)
    acc = jax.ShapeDtypeStruct((m, d), f32)
    vmem = pl.BlockSpec(memory_space=pltpu.VMEM)
    first = gn is None
    args = (n2, dy, b0, b1, ub, br) + (() if first else (gn,))
    return pl.pallas_call(
        functools.partial(ffn_kernel, first),
        out_shape=(acc, acc, block, block, jax.ShapeDtypeStruct((1, 2 * h), f32)),
        in_specs=[vmem] * len(args),
        out_specs=(vmem,) * 5,
        scratch_shapes=[pltpu.VMEM((2 * h, d), bf16)] * 4,
        compiler_params=pltpu.CompilerParams(vmem_limit_bytes=VMEM_BYTES),
        cost_estimate=pl.CostEstimate(
            flops=24 * m * d * h, bytes_accessed=20 * m * d + 16 * h * d, transcendentals=0
        ),
        name="ffn_pair",
    )(*args)


def windows(items):
    out = []
    for i in range(items):
        lo, hi = i * SEQ, (i + 1) * SEQ
        out.append((lo // 16 * 16, -(-hi // 16) * 16, lo, hi))
    return out


def key_mask(length, start, stop, lo, hi):
    row = lax.broadcasted_iota(jnp.int32, (1, stop - start), 1) + start
    pos = row - lo
    own = (row >= lo) & (row < hi)
    return own & ((pos < 1) | (pos > CAP) | (pos - 1 < length))


def put(ref, index, start, lo, value):
    stop = start + value.shape[0]
    if start == lo:
        ref[index, start:stop, :] = value
        return
    edge = start + 16
    row = lax.broadcasted_iota(jnp.int32, (16, 1), 0) + start
    kept = ref[index, start:edge, :]
    ref[index, start:edge, :] = jnp.where(row >= lo, value[:16], kept)
    ref[index, edge:stop, :] = value[16:]


def offsets(hw):
    out = []
    for b in range(2):
        for hh in range(hw // HD):
            out.append(
                (
                    b * 2 * hw + hh * HD,
                    b * 2 * hw + hw + hh * HD,
                    4 * hw + b * hw + hh * HD,
                    b * hw + hh * HD,
                )
            )
    return out


def softmax_parts(q, k, valid):
    s = jnp.where(valid, dot_nt(q, k), MASKED)
    top = jnp.max(s, -1, keepdims=True)
    e = jnp.exp((s - top) * HD ** (-0.5))
    return e * (1.0 / jnp.sum(e, -1, keepdims=True))


def load_pair(b0, b1, wq, wo):
    hw = b0.shape[0] // 4
    wq[: 2 * hw], wq[2 * hw : 4 * hw] = b0[: 2 * hw], b1[: 2 * hw]
    wq[4 * hw : 5 * hw], wq[5 * hw :] = b0[2 * hw : 3 * hw], b1[2 * hw : 3 * hw]
    wo[:hw], wo[hw:] = b0[3 * hw :], b1[3 * hw :]


def attend_kernel(items, lens, normed, b0, b1, acc_in, acc, qkv, mixed, wq, wo, slab, oslab):
    hw = b0.shape[0] // 4
    heads = 2 * hw // HD
    load_pair(b0, b1, wq, wo)
    qkv[...] = dot_nt(normed[...], wq[...]).astype(bf16)
    places = offsets(hw)
    for n, place in enumerate(places):
        for part in range(3):
            slab[part * heads + n] = qkv[:, place[part] : place[part] + HD]

    def step(n, carry):
        for i, (start, stop, lo, hi) in enumerate(windows(items)):
            valid = key_mask(lens[i], start, stop, lo, hi)
            q = slab[n, start:stop, :]
            k = slab[heads + n, start:stop, :]
            v = slab[2 * heads + n, start:stop, :]
            prob = softmax_parts(q, k, valid).astype(bf16)
            put(oslab, n, start, lo, dot_nn(prob, v).astype(bf16))
        return carry

    lax.fori_loop(0, heads, step, 0)
    for n, place in enumerate(places):
        mixed[:, place[3] : place[3] + HD] = oslab[n]
    acc[...] = acc_in[...] + dot_nn(mixed[...], wo[...])


def attend_pair(lens, normed, b0, b1, acc):
    m, d = normed.shape
    hw = b0.shape[0] // 4
    heads = 2 * hw // HD
    items = m // SEQ
    vmem = pl.BlockSpec(memory_space=pltpu.VMEM)
    return pl.pallas_call(
        functools.partial(attend_kernel, items),
        out_shape=(
            jax.ShapeDtypeStruct((m, d), f32),
            jax.ShapeDtypeStruct((m, 6 * hw), bf16),
            jax.ShapeDtypeStruct((m, 2 * hw), bf16),
        ),
        in_specs=[pl.BlockSpec(memory_space=pltpu.SMEM)] + [vmem] * 4,
        out_specs=(vmem,) * 3,
        scratch_shapes=[
            pltpu.VMEM((6 * hw, d), bf16),
            pltpu.VMEM((2 * hw, d), bf16),
            pltpu.VMEM((3 * heads, m, HD), bf16),
            pltpu.VMEM((heads, m, HD), bf16),
        ],
        compiler_params=pltpu.CompilerParams(vmem_limit_bytes=VMEM_BYTES),
        cost_estimate=pl.CostEstimate(
            flops=16 * m * d * hw + 4 * heads * m * SEQ * 256,
            bytes_accessed=10 * m * d + 16 * hw * d + 16 * m * hw,
            transcendentals=0,
        ),
        name="attend_pair",
    )(lens, normed, b0, b1, acc)


def attend_back_kernel(
    items, first, lens, normed, ga, b0, b1, qkv, mixed, *rest
):
    if first:
        gn_in = None
        gn, g0, g1, wq, wo, slab, gslab, gt = rest
    else:
        gn_in, gn, g0, g1, wq, wo, slab, gslab, gt = rest
    hw = b0.shape[0] // 4
    heads = 2 * hw // HD
    load_pair(b0, b1, wq, wo)
    grad_mixed = dot_nt(ga[...], wo[...]).astype(bf16)
    places = offsets(hw)
    for n, place in enumerate(places):
        for part in range(3):
            slab[part * heads + n] = qkv[:, place[part] : place[part] + HD]
        slab[3 * heads + n] = grad_mixed[:, place[3] : place[3] + HD]
    scale = HD ** (-0.5)

    def step(n, carry):
        for i, (start, stop, lo, hi) in enumerate(windows(items)):
            valid = key_mask(lens[i], start, stop, lo, hi)
            row = lax.broadcasted_iota(jnp.int32, (stop - start, 1), 0) + start
            q = slab[n, start:stop, :]
            k = slab[heads + n, start:stop, :]
            v = slab[2 * heads + n, start:stop, :]
            go = slab[3 * heads + n, start:stop, :].astype(f32)
            go = jnp.where((row >= lo) & (row < hi), go, 0.0).astype(bf16)
            prob = softmax_parts(q, k, valid)
            grad_prob = dot_nt(go, v)
            inner = jnp.sum(prob * grad_prob, -1, keepdims=True)
            grad_score = (prob * (grad_prob - inner)).astype(bf16)
            put(gslab, n, start, lo, (dot_nn(grad_score, k) * scale).astype(bf16))
            put(gslab, heads + n, start, lo, (dot_tn(grad_score, q) * scale).astype(bf16))
            put(gslab, 2 * heads + n, start, lo, dot_tn(prob.astype(bf16), go).astype(bf16))
        return carry

    lax.fori_loop(0, heads, step, 0)
    for n, place in enumerate(places):
        for part in range(3):
            gt[:, place[part] : place[part] + HD] = gslab[part * heads + n]
    total = dot_nn(gt[...], wq[...])
    gn[...] = total if first else gn_in[...] + total
    g0[: 2 * hw] = dot_tn(gt[:, : 2 * hw], normed[...]).astype(bf16)
    g1[: 2 * hw] = dot_tn(gt[:, 2 * hw : 4 * hw], normed[...]).astype(bf16)
    grad_v = dot_tn(gt[:, 4 * hw :], normed[...]).astype(bf16)
    grad_o = dot_tn(mixed[...], ga[...]).astype(bf16)
    g0[2 * hw : 3 * hw], g0[3 * hw :] = grad_v[:hw], grad_o[:hw]
    g1[2 * hw : 3 * hw], g1[3 * hw :] = grad_v[hw:], grad_o[hw:]


def attend_back_pair(lens, normed, ga, b0, b1, qkv, mixed, gn):
    m, d = normed.shape
    hw = b0.shape[0] // 4
    heads = 2 * hw // HD
    items = m // SEQ
    vmem = pl.BlockSpec(memory_space=pltpu.VMEM)
    block = jax.ShapeDtypeStruct((4 * hw, d), bf16)
    first = gn is None
    args = (lens, normed, ga, b0, b1, qkv, mixed) + (() if first else (gn,))
    return pl.pallas_call(
        functools.partial(attend_back_kernel, items, first),
        out_shape=(jax.ShapeDtypeStruct((m, d), f32), block, block),
        in_specs=[pl.BlockSpec(memory_space=pltpu.SMEM)] + [vmem] * (len(args) - 1),
        out_specs=(vmem,) * 3,
        scratch_shapes=[
            pltpu.VMEM((6 * hw, d), bf16),
            pltpu.VMEM((2 * hw, d), bf16),
            pltpu.VMEM((4 * heads, m, HD), bf16),
            pltpu.VMEM((3 * heads, m, HD), bf16),
            pltpu.VMEM((m, 6 * hw), bf16),
        ],
        compiler_params=pltpu.CompilerParams(vmem_limit_bytes=VMEM_BYTES),
        cost_estimate=pl.CostEstimate(
            flops=32 * m * d * hw + 10 * heads * m * SEQ * 256,
            bytes_accessed=12 * m * d + 24 * hw * d + 16 * m * hw,
            transcendentals=0,
        ),
        name="attend_back_pair",
    )(*args)


def norm_parts(values):
    centred = values - jnp.mean(values, -1, keepdims=True)
    inv = lax.rsqrt(jnp.mean(centred * centred, -1, keepdims=True) + EPS)
    return centred * inv, inv


def norm_back(unit, inv, gain, grad):
    e = grad * gain
    return inv * (e - jnp.mean(e, -1, keepdims=True) - unit * jnp.mean(e * unit, -1, keepdims=True))


def swap(value, bit, size):
    return lax.ppermute(value, "mp", [(i, i ^ bit) for i in range(size)])


def orders(size):
    bits = [1 << n for n in range(1, size.bit_length() - 1)]
    return bits + [1], bits[::-1] + [1]


def gather_blocks(block, order, size):
    blocks = {0: block}
    for bit in order:
        for j in list(blocks):
            blocks[j | bit] = swap(blocks[j], bit, size)
    return blocks


def add(*values):
    return functools.reduce(jnp.add, [v.astype(f32) for v in values])


def scatter_blocks(blocks, order, size):
    blocks = dict(blocks)
    for bit in reversed(order):
        for j in sorted(blocks, reverse=True):
            if j & bit:
                got = swap(blocks.pop(j), bit, size)
                blocks[j ^ bit] = add(blocks[j ^ bit], got).astype(bf16)
    return blocks[0]


def core_sums(blocks, size):
    out = {}
    for j in sorted(blocks, reverse=True):
        if j & 1:
            got = swap(blocks[j], 1, size)
            out[j ^ 1] = add(blocks[j ^ 1], got).astype(bf16)
    return out


def line_gather(value):
    n, z = lax.axis_size("dp"), lax.axis_index("dp")
    bit = 1
    while bit < n:
        other = lax.ppermute(value, "dp", [(i, i ^ bit) for i in range(n)])
        high = (z & bit) != 0
        value = jnp.concatenate(
            [jnp.where(high, other, value), jnp.where(high, value, other)], 0
        )
        bit *= 2
    return value


def line_scatter(blocks):
    n, z = lax.axis_size("dp"), lax.axis_index("dp")
    bit = n // 2
    while bit:
        place = jnp.where((z & bit) != 0, bit, 0)
        kept = lax.dynamic_slice_in_dim(blocks, place, bit, 0)
        sent = lax.dynamic_slice_in_dim(blocks, bit - place, bit, 0)
        got = lax.ppermute(sent, "dp", [(i, i ^ bit) for i in range(n)])
        blocks = add(kept, got)
        bit //= 2
        if bit:
            blocks = blocks.astype(bf16)
    return blocks[0]


def shards(
    tokens,
    skip_tokens,
    caption_lengths,
    output_cotangent,
    skip_weight,
    norm_gains,
    bias_rows,
    input_weight,
    output_weight,
    up_weight,
    up_bias,
    down_weight,
):
    dp, mp = lax.axis_size("dp"), lax.axis_size("mp")
    my = lax.axis_index("mp")
    rows, d = tokens.shape
    items = rows // SEQ
    m = -(-rows // 16) * 16
    hw = input_weight.shape[2]
    part = skip_weight.shape[0]
    cols = norm_gains.shape[1]
    hidden_part = up_bias.shape[0]
    h = up_weight.shape[1]
    order_a, order_b = orders(mp)

    vector = jnp.concatenate([norm_gains.reshape(-1), bias_rows.reshape(-1), up_bias])
    vector = jnp.pad(vector, (0, d - vector.shape[0])).reshape(1, d)
    extra = jnp.pad(vector, ((0, 7), (0, 0)))
    packed = jnp.concatenate([skip_weight, extra], 0)
    span = packed.shape[0]
    skip_block = line_gather(packed)
    attn_part = jnp.concatenate([input_weight.reshape(-1, 3 * hw), output_weight.T], 1)
    attn_block = line_gather(attn_part).T
    ffn_part = jnp.concatenate([up_weight, down_weight.T], 1)
    ffn_block = line_gather(ffn_part).T

    skip = gather_blocks(skip_block, order_a[:-1], mp)
    own_core = jnp.stack([skip[j] for j in sorted(skip)])
    other_core = swap(own_core, 1, mp)
    attn = gather_blocks(attn_block, order_a, mp)
    ffn = gather_blocks(ffn_block, order_b, mp)

    whole_skip = jnp.zeros((dp, mp, part, d), bf16)
    whole_vec = jnp.zeros((dp, mp, 7, cols), bf16)
    shifts_up = {}
    for j in range(mp):
        piece = (other_core if j & 1 else own_core)[j // 2].reshape(dp, span, d)
        whole_skip = lax.dynamic_update_slice(
            whole_skip, piece[:, None, :part], (0, my ^ j, 0, 0)
        )
        line = piece[:, part]
        whole_vec = lax.dynamic_update_slice(
            whole_vec, line[:, : 7 * cols].reshape(dp, 1, 7, cols), (0, my ^ j, 0, 0)
        )
        shifts_up[j] = line[:, 7 * cols : 7 * cols + hidden_part].reshape(1, -1).astype(f32)
    whole_skip = whole_skip.reshape(2 * d, d)
    vectors = whole_vec.transpose(2, 0, 1, 3).reshape(7, d).astype(f32)
    gains, shift = vectors[:2], vectors[2:]

    pad = ((0, m - rows), (0, 0))
    tok, skp, dy = jnp.pad(tokens, pad), jnp.pad(skip_tokens, pad), jnp.pad(output_cotangent, pad)
    lens = lax.dynamic_slice(caption_lengths, (my * items,), (items,))
    joined = jnp.concatenate([tok, skp], 1)
    hidden = jnp.dot(joined, whole_skip, preferred_element_type=f32) + shift[0]
    unit_one, inv_one = norm_parts(hidden)
    normed = (unit_one * gains[0] + shift[1]).astype(bf16)

    middle = hidden + shift[2]
    kept = {}
    pairs = [0, *range(2, mp, 2)]
    for j in pairs:
        middle, qkv, mixed = attend_pair(lens, normed, attn[j], attn[j + 1], middle)
        kept[j] = (qkv, mixed)
    unit_two, inv_two = norm_parts(middle)
    normed_two = (unit_two * gains[1] + shift[3]).astype(bf16)

    result, grad_two = middle + shift[4], None
    grad_ffn, grad_up_bias = {}, {}
    for j in pairs:
        ub = jnp.concatenate([shifts_up[j], shifts_up[j + 1]], 1)
        result, grad_two, grad_ffn[j], grad_ffn[j + 1], gub = ffn_pair(
            normed_two, dy, ffn[j], ffn[j + 1], ub, result, grad_two
        )
        gub = gub.reshape(2, dp, hidden_part)
        grad_up_bias[j], grad_up_bias[j + 1] = gub[0], gub[1]
    output = result[:rows].astype(bf16)
    chip_ffn = core_sums(grad_ffn, mp)
    own_up = scatter_blocks({j: v[:h] for j, v in chip_ffn.items()}, order_a[:-1], mp)
    own_down = scatter_blocks({j: v[h:] for j, v in chip_ffn.items()}, order_b[:-1], mp)
    own_ffn = jnp.concatenate([own_up, own_down], 0)
    ffn_grads = line_scatter(own_ffn.T.reshape(dp, -1, 2 * h))
    up_grads, down_grads = ffn_grads[:, :h], ffn_grads[:, h:].T

    dy32 = dy.astype(f32)
    grad_middle = dy32 + norm_back(unit_two, inv_two, gains[1], grad_two)
    grad_attention = grad_middle.astype(bf16)

    grad_one = None
    grad_attn = {}
    for j in reversed(pairs):
        grad_one, grad_attn[j], grad_attn[j + 1] = attend_back_pair(
            lens, normed, grad_attention, attn[j], attn[j + 1], *kept[j], grad_one
        )
    own_attn = scatter_blocks(grad_attn, order_a, mp)
    attn_grads = line_scatter(own_attn.T.reshape(dp, -1, 4 * hw))
    in_grads = attn_grads[:, : 3 * hw].reshape(-1, 3, hw)
    out_grads = attn_grads[:, 3 * hw :].T

    grad_hidden = (grad_middle + norm_back(unit_one, inv_one, gains[0], grad_one)).astype(bf16)
    grad_skip = lax.dot_general(
        joined, grad_hidden, (((0,), (0,)), ((), ())), preferred_element_type=f32
    ).astype(bf16)
    grad_tok = dot_nt(grad_hidden, whole_skip[:d])[:rows].astype(bf16)
    grad_skp = dot_nt(grad_hidden, whole_skip[d:])[:rows].astype(bf16)
    vector_grads = jnp.stack(
        [
            jnp.sum(grad_one * unit_one, 0),
            jnp.sum(grad_two * unit_two, 0),
            jnp.sum(grad_hidden.astype(f32), 0),
            jnp.sum(grad_one, 0),
            jnp.sum(grad_attention.astype(f32), 0),
            jnp.sum(grad_two, 0),
            jnp.sum(dy32, 0),
        ]
    )
    vector_grads = vector_grads.reshape(7, dp, mp, cols).transpose(2, 1, 0, 3)
    vector_grads = vector_grads.reshape(mp, dp, 7 * cols)
    grad_skip = grad_skip.reshape(dp, mp, part, d)
    pieces = []
    for j in range(mp):
        piece = lax.dynamic_slice(grad_skip, (0, my ^ j, 0, 0), (dp, 1, part, d))[:, 0]
        line = lax.dynamic_slice(vector_grads, (my ^ j, 0, 0), (1, dp, 7 * cols))[0]
        line = jnp.concatenate([line, grad_up_bias[j]], 1)
        line = jnp.pad(line[:, None], ((0, 0), (0, 7), (0, d - line.shape[1]))).astype(bf16)
        pieces.append(jnp.concatenate([piece, line], 1).reshape(dp * span, d))
    got = swap(jnp.stack(pieces[1::2]), 1, mp)
    tail = {2 * n: add(pieces[2 * n], got[n]).astype(bf16) for n in range(mp // 2)}
    tail = scatter_blocks(tail, order_a[:-1], mp)
    tail = line_scatter(tail.reshape(dp, span, d))
    skip_grads = tail[:part]
    line = tail[part]
    gain_grads = line[: 2 * cols].reshape(2, cols)
    shift_grads = line[2 * cols : 7 * cols].reshape(5, cols)
    up_bias_grads = line[7 * cols : 7 * cols + hidden_part]
    return (
        output,
        grad_tok,
        grad_skp,
        skip_grads,
        gain_grads,
        shift_grads,
        in_grads,
        out_grads,
        up_grads,
        up_bias_grads,
        down_grads,
    )


def solution(mesh):
    both = P(("dp", "mp"), None)
    last = P(None, ("dp", "mp"))
    in_specs = (
        both, both, P("dp"), both, both, last, last,
        P("dp", None, "mp"), P("mp", "dp"), P("dp", "mp"), P(("mp", "dp")), P("mp", "dp"),
    )
    out_specs = (
        both, both, both, both, last, last,
        P("dp", None, "mp"), P("mp", "dp"), P("dp", "mp"), P(("mp", "dp")), P("mp", "dp"),
    )
    return jax.shard_map(shards, mesh=mesh, in_specs=in_specs, out_specs=out_specs, check_vma=False)
```

time: 1340 us -> 869 us (0.65)
  blocking collectives: 540 us -> 0 us
  matrix products: 278 us -> 21.9 us
  Pallas kernels: 0 us -> 232 us
  waiting for transfers between devices: 269 us -> 405 us
  local copies, waits for them, and re-layouts: 177 us -> 71.7 us
  starting transfers between devices: 3.36 us -> 44.4 us
  other arithmetic: 42.8 us -> 83.3 us
  between operations: 18.3 us -> 2.31 us
    ppermute x0 -> x51, waiting for transfers between devices: none -> 405 us  [the longest x39 225 us: swap(): return lax.ppermute(value, 'mp', [(i, i ^ bit) for i in range(size)])]
    unnamed x7 -> x0, blocking collectives: 375 us -> none
    dot_general x71 -> x4, matrix products: 278 us -> 21.9 us  [the longest x1 7.72 us: shards(): hidden = jnp.dot(joined, whole_skip, preferred_element_type=f32) + shift[0]]
    pallas_call x0 -> x12, Pallas kernels: none -> 232 us  [the longest x4 106 us: ffn_pair(): pl.pallas_call(functools.partial(ffn_kernel, first), out_shape=(acc, acc,...]
    all_gather x4 -> x0, blocking collectives: 165 us -> none  [the longest x1 69.1 us: shards(): lax.all_gather(input_weight, 'dp', axis=0, tiled=True)]
    all_gather x7 -> x0, waiting for transfers between devices: 113 us -> none  [the longest x1 71 us: shards(): attention_rows = lax.all_gather(grad_attention, 'mp', axis=0, tiled=True)]
    reduce_scatter x2 -> x0, waiting for transfers between devices: 106 us -> none  [the longest x1 72.4 us: shards(): lax.psum_scatter(grad_down_whole.astype(jnp.bfloat16), 'mp', scatter_dime...]
    unnamed x113 -> x105, local copies, waits for them, and re-layouts: 88.2 us -> 8.35 us
  transfers between devices with their start and end apart: 16 -> 51, of which waited for: 6 -> 17; matrix products, arithmetic and copies ran while one was open for 52% -> 19% of each run, Pallas kernels for 0% -> 27%
where the time goes in v1:
time: 869 us; the launch traced here: 860 us
  waiting for transfers between devices  405 us (47%)
  Pallas kernels  232 us (27%)
  other arithmetic  83.3 us (10%)
  local copies, waits for them, and re-layouts  71.7 us (8%)
  starting transfers between devices  44.4 us (5%)
  matrix products  21.9 us (3%)
    ppermute x39, waiting for transfers between devices, swap(): return lax.ppermute(value, 'mp', [(i, i ^ bit) for i in range(size)])  225 us
    pallas_call x4, Pallas kernels, ffn_pair(): pl.pallas_call(functools.partial(ffn_kernel, first), out_shape=(acc, acc,...  106 us
    ppermute x6, waiting for transfers between devices, line_scatter(): got = lax.ppermute(sent, 'dp', [(i, i ^ bit) for i in range(n)])  95.4 us
    ppermute x6, waiting for transfers between devices, line_gather(): other = lax.ppermute(value, 'dp', [(i, i ^ bit) for i in range(n)])  83.8 us
    pallas_call x4, Pallas kernels, attend_back_pair(): pl.pallas_call(functools.partial(attend_back_kernel, items, first), out_s...  75.1 us
    pallas_call x4, Pallas kernels, attend_pair(): pl.pallas_call(functools.partial(attend_kernel, items), out_shape=(jax.Sh...  50.6 us
    ppermute x39, starting transfers between devices, swap(): return lax.ppermute(value, 'mp', [(i, i ^ bit) for i in range(size)])  27.8 us
  transfers between devices with their start and end apart: 51, of which 17 were waited for; matrix products, arithmetic and copies ran while one was open for 19% of the time, Pallas kernels for 27%

profile of v1, /device:TPU:0, one launch (start us, length us, event | category | flops | bytes accessed | tf_op | source)
XLA Modules:
  0.0 860.0 jit_solution(18172630813555841564)
XLA Ops:
  3.9 3.1 collective-permute-start
  7.0 4.6 collective-permute-done
  12.6 2.8 collective-permute-start.1
  15.5 15.8 %collective-permute-done.1 = bf16[160,1152]{1,0:T(8,128)(2,1)S(1)} collective-permute-done((bf16[160,1152]{1,0:T(8,128)(2,1)S(1)}, bf16[160,1152]{1,0:T(8,128)(2,1)S(1)}, u32[]{:S(2)}, u32[]{:S(2)}) %collective-permute-start.1) | collective-permute-done | bytes 368672 | tf_op jit(solution)/shard_map/ppermute | solution.py:362
  37.6 12.6 %collective-permute-done.2 = bf16[320,1152]{1,0:T(8,128)(2,1)} collective-permute-done((bf16[320,1152]{1,0:T(8,128)(2,1)}, bf16[320,1152]{1,0:T(8,128)(2,1)}, u32[]{:S(2)}, u32[]{:S(2)}) %collective-permute-start.2) | collective-permute-done | bytes 737312 | tf_op jit(solution)/shard_map/ppermute | solution.py:319
  57.5 3.4 collective-permute-start.7
  60.9 18.6 %collective-permute-done.15 = bf16[288,1152]{1,0:T(8,128)(2,1)S(1)} collective-permute-done((bf16[288,1152]{1,0:T(8,128)(2,1)}, bf16[288,1152]{1,0:T(8,128)(2,1)S(1)}, u32[]{:S(2)}, u32[]{:S(2)}) %collective-permute-start.15) | collective-permute-done | bytes 663584 | tf_op jit(solution)/shard_map/ppermute | solution.py:362
  79.9 3.1 pad_maximum_fusion
  90.5 30.6 %collective-permute-done.7 = bf16[576,576]{0,1:T(8,128)(2,1)} collective-permute-done((bf16[576,576]{0,1:T(8,128)(2,1)}, bf16[576,576]{0,1:T(8,128)(2,1)}, u32[]{:S(2)}, u32[]{:S(2)}) %collective-permute-start.7) | collective-permute-done | bytes 663584 | tf_op jit(solution)/shard_map/ppermute | solution.py:362
  125.9 2.8 broadcast_in_dim.70
  135.0 14.1 %collective-permute-done.16 = bf16[576,1152]{1,0:T(8,128)(2,1)} collective-permute-done((bf16[576,1152]{1,0:T(8,128)(2,1)}, bf16[576,1152]{1,0:T(8,128)(2,1)}, u32[]{:S(2)}, u32[]{:S(2)}) %collective-permute-start.16) | collective-permute-done | bytes 1327136 | tf_op jit(solution)/shard_map/ppermute | solution.py:362
  172.5 7.7 fusion.60
  182.1 67.1 %collective-permute-done.9.b0 = bf16[576,1152]{1,0:T(8,128)(2,1)} collective-permute-done((bf16[576,1152]{1,0:T(8,128)(2,1)}, bf16[576,1152]{1,0:T(8,128)(2,1)}, u32[]{:S(2)}, u32[]{:S(2)}) %collective-permute-start.9) | collective-permute-done | bytes 1327136 | tf_op jit(solution)/shard_map/ppermute | solution.py:319
  249.3 2.9 broadcast_add_fusion.1
  252.7 12.9 %attend_pair.4 = (f32[672,1152]{1,0:T(8,128)}, bf16[672,864]{1,0:T(8,128)(2,1)}, bf16[672,288]{1,0:T(8,128)(2,1)}) custom-call(s32[2]{0:T(128)} %dynamic_slice.87.lens, bf16[672,1152]{1,0:T(8,128)(2,1)} %get-tuple-element.166.normed, bf16[576,1152]{1,0:T(8,128)(2,1)} %maximum_bitcast_fusion.2.b0, bf16[576,1152]{1,0:T(8,128)(2,1)} %collective-permute-done.14.b1, ...), custom_call_target="tpu_custom_call" | custom-call | flops 2702966784 | bytes 11943936 | tf_op jit(solution)/shard_map/attend_pair/pallas_call | solution.py:200
  265.6 12.5 %attend_pair.5 = (f32[672,1152]{1,0:T(8,128)}, bf16[672,864]{1,0:T(8,128)(2,1)}, bf16[672,288]{1,0:T(8,128)(2,1)}) custom-call(s32[2]{0:T(128)} %dynamic_slice.87.lens, bf16[672,1152]{1,0:T(8,128)(2,1)} %get-tuple-element.166.normed, bf16[576,1152]{1,0:T(8,128)(2,1)} %collective-permute-done.8.b0, bf16[576,1152]{1,0:T(8,128)(2,1)} %collective-permute-done.13.b1, ...), custom_call_target="tpu_custom_call" | custom-call | flops 2702966784 | bytes 11943936 | tf_op jit(solution)/shard_map/attend_pair/pallas_call | solution.py:200
  278.8 12.5 %attend_pair.6 = (f32[672,1152]{1,0:T(8,128)}, bf16[672,864]{1,0:T(8,128)(2,1)}, bf16[672,288]{1,0:T(8,128)(2,1)}) custom-call(s32[2]{0:T(128)} %dynamic_slice.87.lens, bf16[672,1152]{1,0:T(8,128)(2,1)} %get-tuple-element.166.normed, bf16[576,1152]{1,0:T(8,128)(2,1)} %collective-permute-done.11.b0, bf16[576,1152]{1,0:T(8,128)(2,1)} %collective-permute-done.12.b1, ...), custom_call_target="tpu_custom_call" | custom-call | flops 2702966784 | bytes 11943936 | tf_op jit(solution)/shard_map/attend_pair/pallas_call | solution.py:200
  291.3 12.7 %attend_pair.7 = (f32[672,1152]{1,0:T(8,128)}, bf16[672,864]{1,0:T(8,128)(2,1)}, bf16[672,288]{1,0:T(8,128)(2,1)}) custom-call(s32[2]{0:T(128)} %dynamic_slice.87.lens, bf16[672,1152]{1,0:T(8,128)(2,1)} %get-tuple-element.166.normed, bf16[576,1152]{1,0:T(8,128)(2,1)} %collective-permute-done.9.b0, bf16[576,1152]{1,0:T(8,128)(2,1)} %collective-permute-done.10.b1, ...), custom_call_target="tpu_custom_call" | custom-call | flops 2702966784 | bytes 11943936 | tf_op jit(solution)/shard_map/attend_pair/pallas_call | solution.py:200
  307.2 2.9 broadcast_add_fusion
  310.8 25.8 %ffn_pair.4 = (f32[672,1152]{1,0:T(8,128)}, f32[672,1152]{1,0:T(8,128)}, bf16[1152,1152]{1,0:T(8,128)(2,1)}, bf16[1152,1152]{1,0:T(8,128)(2,1)}, f32[1,1152]{1,0:T(1,128)}) custom-call(bf16[672,1152]{1,0:T(8,128)(2,1)} %get-tuple-element.164.n2, bf16[672,1152]{1,0:T(8,128)(2,1)} %pad.55.dy, bf16[1152,1152]{1,0:T(8,128)(2,1)} %maximum_bitcast_fusion.b0, ...), custom_call_target="tpu_custom_call" | custom-call | flops 10701766656 | bytes 26099712 | tf_op jit(solution)/shard_map/ffn_pair/pallas_call | solution.py:98
  339.1 5.3 fusion.56
  345.9 26.7 %ffn_pair.5 = (f32[672,1152]{1,0:T(8,128)}, f32[672,1152]{1,0:T(8,128)}, bf16[1152,1152]{1,0:T(8,128)(2,1)}, bf16[1152,1152]{1,0:T(8,128)(2,1)}, f32[1,1152]{1,0:T(1,128)}) custom-call(bf16[672,1152]{1,0:T(8,128)(2,1)} %get-tuple-element.164.n2, bf16[672,1152]{1,0:T(8,128)(2,1)} %pad.55.dy, bf16[1152,1152]{1,0:T(8,128)(2,1)} %collective-permute-done.21.b0, ...), custom_call_target="tpu_custom_call" | custom-call | flops 10701766656 | bytes 26099712 | tf_op jit(solution)/shard_map/ffn_pair/pallas_call | solution.py:98
  372.6 26.9 %ffn_pair.6 = (f32[672,1152]{1,0:T(8,128)}, f32[672,1152]{1,0:T(8,128)}, bf16[1152,1152]{1,0:T(8,128)(2,1)}, bf16[1152,1152]{1,0:T(8,128)(2,1)}, f32[1,1152]{1,0:T(1,128)}) custom-call(bf16[672,1152]{1,0:T(8,128)(2,1)} %get-tuple-element.164.n2, bf16[672,1152]{1,0:T(8,128)(2,1)} %pad.55.dy, bf16[1152,1152]{1,0:T(8,128)(2,1)} %collective-permute-done.17.b0, ...), custom_call_target="tpu_custom_call" | custom-call | flops 10701766656 | bytes 26099712 | tf_op jit(solution)/shard_map/ffn_pair/pallas_call | solution.py:98
  401.3 4.7 add_convert_fusion.3
  406.0 26.6 %ffn_pair.7 = (f32[672,1152]{1,0:T(8,128)}, f32[672,1152]{1,0:T(8,128)}, bf16[1152,1152]{1,0:T(8,128)(2,1)}, bf16[1152,1152]{1,0:T(8,128)(2,1)}, f32[1,1152]{1,0:T(1,128)}) custom-call(bf16[672,1152]{1,0:T(8,128)(2,1)} %get-tuple-element.164.n2, bf16[672,1152]{1,0:T(8,128)(2,1)} %pad.55.dy, bf16[1152,1152]{1,0:T(8,128)(2,1)} %collective-permute-done.18.b0, ...), custom_call_target="tpu_custom_call" | custom-call | flops 10701766656 | bytes 26099712 | tf_op jit(solution)/shard_map/ffn_pair/pallas_call | solution.py:98
  432.9 3.4 add_convert_fusion.1
  439.2 3.4 convert_reduce_fusion.1
  442.5 17.8 %attend_back_pair.4 = (f32[672,1152]{1,0:T(8,128)}, bf16[576,1152]{1,0:T(8,128)(2,1)}, bf16[576,1152]{1,0:T(8,128)(2,1)}) custom-call(s32[2]{0:T(128)} %dynamic_slice.87.lens, bf16[672,1152]{1,0:T(8,128)(2,1)} %get-tuple-element.166.normed, bf16[672,1152]{1,0:T(8,128)(2,1)} %get-tuple-element.149.ga, bf16[576,1152]{1,0:T(8,128)(2,1)} %collective-permute-done.9.b0, ...), custom_call_target="tpu_custom_call" | custom-call | flops 5865603072 | bytes 14819328 | tf_op jit(solution)/shard_map/attend_back_pair/pallas_call | solution.py:285
  460.3 19.3 %attend_back_pair.5 = (f32[672,1152]{1,0:T(8,128)}, bf16[576,1152]{1,0:T(8,128)(2,1)}, bf16[576,1152]{1,0:T(8,128)(2,1)}) custom-call(s32[2]{0:T(128)} %dynamic_slice.87.lens, bf16[672,1152]{1,0:T(8,128)(2,1)} %get-tuple-element.166.normed, bf16[672,1152]{1,0:T(8,128)(2,1)} %get-tuple-element.149.ga, bf16[576,1152]{1,0:T(8,128)(2,1)} %collective-permute-done.11.b0, ...), custom_call_target="tpu_custom_call" | custom-call | flops 5865603072 | bytes 14819328 | tf_op jit(solution)/shard_map/attend_back_pair/pallas_call | solution.py:285
  480.1 18.9 %attend_back_pair.6 = (f32[672,1152]{1,0:T(8,128)}, bf16[576,1152]{1,0:T(8,128)(2,1)}, bf16[576,1152]{1,0:T(8,128)(2,1)}) custom-call(s32[2]{0:T(128)} %dynamic_slice.87.lens, bf16[672,1152]{1,0:T(8,128)(2,1)} %get-tuple-element.166.normed, bf16[672,1152]{1,0:T(8,128)(2,1)} %get-tuple-element.149.ga, bf16[576,1152]{1,0:T(8,128)(2,1)} %collective-permute-done.8.b0, ...), custom_call_target="tpu_custom_call" | custom-call | flops 5865603072 | bytes 14819328 | tf_op jit(solution)/shard_map/attend_back_pair/pallas_call | solution.py:285
  499.2 19.2 %attend_back_pair.7 = (f32[672,1152]{1,0:T(8,128)}, bf16[576,1152]{1,0:T(8,128)(2,1)}, bf16[576,1152]{1,0:T(8,128)(2,1)}) custom-call(s32[2]{0:T(128)} %dynamic_slice.87.lens, bf16[672,1152]{1,0:T(8,128)(2,1)} %get-tuple-element.166.normed, bf16[672,1152]{1,0:T(8,128)(2,1)} %get-tuple-element.149.ga, bf16[576,1152]{1,0:T(8,128)(2,1)} %maximum_bitcast_fusion.2.b0, ...), custom_call_target="tpu_custom_call" | custom-call | flops 5865603072 | bytes 14819328 | tf_op jit(solution)/shard_map/attend_back_pair/pallas_call | solution.py:285
  518.4 3.1 multiply_reduce_fusion.1
  521.8 4.3 convert_reduce_fusion.2
  527.9 7.1 convolution_convert_fusion
  544.7 3.5 fusion.62
  550.8 3.5 fusion.61
  557.6 24.6 %collective-permute-done.35 = bf16[576,1152]{1,0:T(8,128)(2,1)S(1)} collective-permute-done((bf16[576,1152]{1,0:T(8,128)(2,1)S(1)}, bf16[576,1152]{1,0:T(8,128)(2,1)S(1)}, u32[]{:S(2)}, u32[]{:S(2)}) %collective-permute-start.35) | collective-permute-done | bytes 1327136 | tf_op jit(solution)/shard_map/ppermute | solution.py:319
  592.8 61.3 %collective-permute-done.26 = bf16[320,1152]{1,0:T(8,128)(2,1)S(1)} collective-permute-done((bf16[320,1152]{1,0:T(8,128)(2,1)S(1)}, bf16[320,1152]{1,0:T(8,128)(2,1)S(1)}, u32[]{:S(2)}, u32[]{:S(2)}) %collective-permute-start.26) | collective-permute-done | bytes 737312 | tf_op jit(solution)/shard_map/ppermute | solution.py:319
  661.1 25.0 %collective-permute-done.47 = bf16[576,1152]{1,0:T(8,128)(2,1)S(1)} collective-permute-done((bf16[576,1152]{1,0:T(8,128)(2,1)S(1)}, bf16[576,1152]{1,0:T(8,128)(2,1)S(1)}, u32[]{:S(2)}, u32[]{:S(2)}) %collective-permute-start.47) | collective-permute-done | bytes 1327136 | tf_op jit(solution)/shard_map/ppermute | solution.py:319
  689.1 2.8 copy.115
  694.1 11.3 %collective-permute-done.25 = bf16[320,1152]{1,0:T(8,128)(2,1)} collective-permute-done((bf16[320,1152]{1,0:T(8,128)(2,1)}, bf16[320,1152]{1,0:T(8,128)(2,1)}, u32[]{:S(2)}, u32[]{:S(2)}) %collective-permute-start.25) | collective-permute-done | bytes 737312 | tf_op jit(solution)/shard_map/ppermute | solution.py:319
  707.1 23.4 %collective-permute-done.27 = bf16[320,1152]{1,0:T(8,128)(2,1)} collective-permute-done((bf16[320,1152]{1,0:T(8,128)(2,1)}, bf16[320,1152]{1,0:T(8,128)(2,1)}, u32[]{:S(2)}, u32[]{:S(2)}) %collective-permute-start.27) | collective-permute-done | bytes 737312 | tf_op jit(solution)/shard_map/ppermute | solution.py:319
  732.4 29.9 %collective-permute-done.37 = bf16[2,288,576]{2,1,0:T(8,128)(2,1)S(1)} collective-permute-done((bf16[2,288,576]{2,1,0:T(8,128)(2,1)S(1)}, bf16[2,288,576]{2,1,0:T(8,128)(2,1)S(1)}, u32[]{:S(2)}, u32[]{:S(2)}) %collective-permute-start.37) | collective-permute-done | bytes 663584 | tf_op jit(solution)/shard_map/ppermute | solution.py:378
  769.0 4.1 copy.117
  776.2 5.0 collective-permute-done.28
  789.8 21.4 %collective-permute-done.29 = bf16[1,80,1152]{2,1,0:T(8,128)(2,1)} collective-permute-done((bf16[1,80,1152]{2,1,0:T(8,128)(2,1)}, bf16[1,80,1152]{2,1,0:T(8,128)(2,1)}, u32[]{:S(2)}, u32[]{:S(2)}) %collective-permute-start.29) | collective-permute-done | bytes 184352 | tf_op jit(solution)/shard_map/ppermute | solution.py:378
  812.9 24.4 %collective-permute-done.49 = bf16[2,288,1152]{2,1,0:T(8,128)(2,1)} collective-permute-done((bf16[2,288,1152]{2,1,0:T(8,128)(2,1)}, bf16[2,288,1152]{2,1,0:T(8,128)(2,1)}, u32[]{:S(2)}, u32[]{:S(2)}) %collective-permute-start.49) | collective-permute-done | bytes 1327136 | tf_op jit(solution)/shard_map/ppermute | solution.py:378
  842.4 14.6 %collective-permute-done.50 = bf16[1,288,1152]{2,1,0:T(8,128)(2,1)S(1)} collective-permute-done((bf16[1,288,1152]{2,1,0:T(8,128)(2,1)S(1)}, bf16[1,288,1152]{2,1,0:T(8,128)(2,1)S(1)}, u32[]{:S(2)}, u32[]{:S(2)}) %collective-permute-start.50) | collective-permute-done | bytes 663584 | tf_op jit(solution)/shard_map/ppermute | solution.py:378
  (386 shorter events, 147.7 us)
Async XLA Ops:
  12.6 18.6 %collective-permute-start.1 = (bf16[160,1152]{1,0:T(8,128)(2,1)S(1)}, bf16[160,1152]{1,0:T(8,128)(2,1)S(1)}, u32[]{:S(2)}, u32[]{:S(2)}) collective-permute-start(bf16[160,1152]{1,0:T(8,128)(2,1)S(1)} %pad_maximum_fusion.7), channel_id=1, source_target_pairs={{0,16},{8,24},{16,0},{24,8},{1,17},{9,25},{17,1},{25,9},{2,18},{10... | collective-permute-start | bytes 1105928 | tf_op jit(solution)/shard_map/ppermute | solution.py:362
  33.8 20.6 %collective-permute-start.6 = (bf16[288,576]{0,1:T(8,128)(2,1)S(1)}, bf16[288,576]{0,1:T(8,128)(2,1)}, u32[]{:S(2)}, u32[]{:S(2)}) collective-permute-start(bf16[288,576]{0,1:T(8,128)(2,1)S(1)} %pad_maximum_fusion.6), channel_id=1, source_target_pairs={{0,8},{8,0},{16,24},{24,16},{1,9},{9,1},{17,25},{25,17},{2,10},{10... | collective-permute-start | bytes 995336 | tf_op jit(solution)/shard_map/ppermute | solution.py:362
  36.0 43.9 %collective-permute-start.3 = (bf16[320,1152]{1,0:T(8,128)(2,1)}, bf16[320,1152]{1,0:T(8,128)(2,1)}, u32[]{:S(2)}, u32[]{:S(2)}) collective-permute-start(bf16[320,1152]{1,0:T(8,128)(2,1)} %get-tuple-element.189), channel_id=1, source_target_pairs={{0,4},{1,5},{2,6},{3,7},{4,0},{5,1},{6,2},{7,3},{8,12},{9,13},{10,... | collective-permute-start | bytes 2211848 | tf_op jit(solution)/shard_map/ppermute | solution.py:319
  50.2 29.7 %collective-permute-start.4 = (bf16[320,1152]{1,0:T(8,128)(2,1)}, bf16[320,1152]{1,0:T(8,128)(2,1)}, u32[]{:S(2)}, u32[]{:S(2)}) collective-permute-start(bf16[320,1152]{1,0:T(8,128)(2,1)} %collective-permute-done.2), channel_id=1, source_target_pairs={{0,4},{1,5},{2,6},{3,7},{4,0},{5,1},{6,2},{7,3},{8,12},{9,13},{10,... | collective-permute-start | bytes 2211848 | tf_op jit(solution)/shard_map/ppermute | solution.py:319
  52.7 26.8 %collective-permute-start.15 = (bf16[288,1152]{1,0:T(8,128)(2,1)}, bf16[288,1152]{1,0:T(8,128)(2,1)S(1)}, u32[]{:S(2)}, u32[]{:S(2)}) collective-permute-start(bf16[288,1152]{1,0:T(8,128)(2,1)} %copy.100), channel_id=1, source_target_pairs={{0,8},{8,0},{16,24},{24,16},{1,9},{9,1},{17,25},{25,17},{2,10},{10... | collective-permute-start | bytes 1990664 | tf_op jit(solution)/shard_map/ppermute | solution.py:362
  57.5 63.6 %collective-permute-start.7 = (bf16[576,576]{0,1:T(8,128)(2,1)}, bf16[576,576]{0,1:T(8,128)(2,1)}, u32[]{:S(2)}, u32[]{:S(2)}) collective-permute-start(bf16[576,576]{0,1:T(8,128)(2,1)} %pad_maximum_fusion.5), channel_id=1, source_target_pairs={{0,16},{8,24},{16,0},{24,8},{1,17},{9,25},{17,1},{25,9},{2,18},{10... | collective-permute-start | bytes 1990664 | tf_op jit(solution)/shard_map/ppermute | solution.py:362
  83.0 74.8 %collective-permute-start.5 = (bf16[4,320,1152]{2,1,0:T(8,128)(2,1)}, bf16[4,320,1152]{2,1,0:T(8,128)(2,1)}, u32[]{:S(2)}, u32[]{:S(2)}) collective-permute-start(bf16[4,320,1152]{2,1,0:T(8,128)(2,1)} %pad_maximum_fusion), channel_id=1, source_target_pairs={{0,1},{1,0},{2,3},{3,2},{4,5},{5,4},{6,7},{7,6},{8,9},{9,8},{10,11... | collective-permute-start | bytes 8847368 | tf_op jit(solution)/shard_map/ppermute | solution.py:319
  87.6 61.6 %collective-permute-start.16 = (bf16[576,1152]{1,0:T(8,128)(2,1)}, bf16[576,1152]{1,0:T(8,128)(2,1)}, u32[]{:S(2)}, u32[]{:S(2)}) collective-permute-start(bf16[576,1152]{1,0:T(8,128)(2,1)} %copy.103), channel_id=1, source_target_pairs={{0,16},{8,24},{16,0},{24,8},{1,17},{9,25},{17,1},{25,9},{2,18},{10... | collective-permute-start | bytes 3981320 | tf_op jit(solution)/shard_map/ppermute | solution.py:362
  124.4 32.8 %collective-permute-start.8 = (bf16[576,1152]{1,0:T(8,128)(2,1)}, bf16[576,1152]{1,0:T(8,128)(2,1)}, u32[]{:S(2)}, u32[]{:S(2)}) collective-permute-start(bf16[576,1152]{1,0:T(8,128)(2,1)} %maximum_bitcast_fusion.2.b0), channel_id=1, source_target_pairs={{0,2},{1,3},{2,0},{3,1},{4,6},{5,7},{6,4},{7,5},{8,10},{9,11},{10,... | collective-permute-start | bytes 3981320 | tf_op jit(solution)/shard_map/ppermute | solution.py:319
  132.0 48.2 %collective-permute-start.14 = (bf16[576,1152]{1,0:T(8,128)(2,1)}, bf16[576,1152]{1,0:T(8,128)(2,1)}, u32[]{:S(2)}, u32[]{:S(2)}) collective-permute-start(bf16[576,1152]{1,0:T(8,128)(2,1)} %maximum_bitcast_fusion.2.b0), channel_id=1, source_target_pairs={{0,1},{1,0},{2,3},{3,2},{4,5},{5,4},{6,7},{7,6},{8,9},{9,8},{10,11... | collective-permute-start | bytes 3981320 | tf_op jit(solution)/shard_map/ppermute | solution.py:319
  132.1 48.7 %collective-permute-start.11 = (bf16[576,1152]{1,0:T(8,128)(2,1)}, bf16[576,1152]{1,0:T(8,128)(2,1)}, u32[]{:S(2)}, u32[]{:S(2)}) collective-permute-start(bf16[576,1152]{1,0:T(8,128)(2,1)} %maximum_bitcast_fusion.2.b0), channel_id=1, source_target_pairs={{0,4},{1,5},{2,6},{3,7},{4,0},{5,1},{6,2},{7,3},{8,12},{9,13},{10,... | collective-permute-start | bytes 3981320 | tf_op jit(solution)/shard_map/ppermute | solution.py:319
  154.6 124.1 %collective-permute-start.21 = (bf16[1152,1152]{1,0:T(8,128)(2,1)}, bf16[1152,1152]{1,0:T(8,128)(2,1)}, u32[]{:S(2)}, u32[]{:S(2)}) collective-permute-start(bf16[1152,1152]{1,0:T(8,128)(2,1)} %maximum_bitcast_fusion.b0), channel_id=1, source_target_pairs={{0,2},{1,3},{2,0},{3,1},{4,6},{5,7},{6,4},{7,5},{8,10},{9,11},{10,... | collective-permute-start | bytes 7962632 | tf_op jit(solution)/shard_map/ppermute | solution.py:319
  157.3 108.3 %collective-permute-start.17 = (bf16[1152,1152]{1,0:T(8,128)(2,1)}, bf16[1152,1152]{1,0:T(8,128)(2,1)}, u32[]{:S(2)}, u32[]{:S(2)}) collective-permute-start(bf16[1152,1152]{1,0:T(8,128)(2,1)} %maximum_bitcast_fusion.b0), channel_id=1, source_target_pairs={{0,4},{1,5},{2,6},{3,7},{4,0},{5,1},{6,2},{7,3},{8,12},{9,13},{10,... | collective-permute-start | bytes 7962632 | tf_op jit(solution)/shard_map/ppermute | solution.py:319
  157.8 91.4 %collective-permute-start.9 = (bf16[576,1152]{1,0:T(8,128)(2,1)}, bf16[576,1152]{1,0:T(8,128)(2,1)}, u32[]{:S(2)}, u32[]{:S(2)}) collective-permute-start(bf16[576,1152]{1,0:T(8,128)(2,1)} %collective-permute-done.8.b0), channel_id=1, source_target_pairs={{0,4},{1,5},{2,6},{3,7},{4,0},{5,1},{6,2},{7,3},{8,12},{9,13},{10,... | collective-permute-start | bytes 3981320 | tf_op jit(solution)/shard_map/ppermute | solution.py:319
  180.3 71.9 %collective-permute-start.13 = (bf16[576,1152]{1,0:T(8,128)(2,1)}, bf16[576,1152]{1,0:T(8,128)(2,1)}, u32[]{:S(2)}, u32[]{:S(2)}) collective-permute-start(bf16[576,1152]{1,0:T(8,128)(2,1)} %collective-permute-done.8.b0), channel_id=1, source_target_pairs={{0,1},{1,0},{2,3},{3,2},{4,5},{5,4},{6,7},{7,6},{8,9},{9,8},{10,11... | collective-permute-start | bytes 3981320 | tf_op jit(solution)/shard_map/ppermute | solution.py:319
  180.8 97.3 %collective-permute-start.12 = (bf16[576,1152]{1,0:T(8,128)(2,1)}, bf16[576,1152]{1,0:T(8,128)(2,1)}, u32[]{:S(2)}, u32[]{:S(2)}) collective-permute-start(bf16[576,1152]{1,0:T(8,128)(2,1)} %collective-permute-done.11.b0), channel_id=1, source_target_pairs={{0,1},{1,0},{2,3},{3,2},{4,5},{5,4},{6,7},{7,6},{8,9},{9,8},{10,11... | collective-permute-start | bytes 3981320 | tf_op jit(solution)/shard_map/ppermute | solution.py:319
  249.3 42.0 %collective-permute-start.10 = (bf16[576,1152]{1,0:T(8,128)(2,1)}, bf16[576,1152]{1,0:T(8,128)(2,1)}, u32[]{:S(2)}, u32[]{:S(2)}) collective-permute-start(bf16[576,1152]{1,0:T(8,128)(2,1)} %collective-permute-done.9.b0), channel_id=1, source_target_pairs={{0,1},{1,0},{2,3},{3,2},{4,5},{5,4},{6,7},{7,6},{8,9},{9,8},{10,11... | collective-permute-start | bytes 3981320 | tf_op jit(solution)/shard_map/ppermute | solution.py:319
  252.1 58.6 %collective-permute-start.23 = (bf16[1152,1152]{1,0:T(8,128)(2,1)}, bf16[1152,1152]{1,0:T(8,128)(2,1)}, u32[]{:S(2)}, u32[]{:S(2)}) collective-permute-start(bf16[1152,1152]{1,0:T(8,128)(2,1)} %maximum_bitcast_fusion.b0), channel_id=1, source_target_pairs={{0,1},{1,0},{2,3},{3,2},{4,5},{5,4},{6,7},{7,6},{8,9},{9,8},{10,11... | collective-permute-start | bytes 7962632 | tf_op jit(solution)/shard_map/ppermute | solution.py:319
  265.6 107.0 %collective-permute-start.20 = (bf16[1152,1152]{1,0:T(8,128)(2,1)}, bf16[1152,1152]{1,0:T(8,128)(2,1)}, u32[]{:S(2)}, u32[]{:S(2)}) collective-permute-start(bf16[1152,1152]{1,0:T(8,128)(2,1)} %collective-permute-done.17.b0), channel_id=1, source_target_pairs={{0,1},{1,0},{2,3},{3,2},{4,5},{5,4},{6,7},{7,6},{8,9},{9,8},{10,11... | collective-permute-start | bytes 7962632 | tf_op jit(solution)/shard_map/ppermute | solution.py:319
  278.1 67.6 %collective-permute-start.18 = (bf16[1152,1152]{1,0:T(8,128)(2,1)}, bf16[1152,1152]{1,0:T(8,128)(2,1)}, u32[]{:S(2)}, u32[]{:S(2)}) collective-permute-start(bf16[1152,1152]{1,0:T(8,128)(2,1)} %collective-permute-done.17.b0), channel_id=1, source_target_pairs={{0,2},{1,3},{2,0},{3,1},{4,6},{5,7},{6,4},{7,5},{8,10},{9,11},{10,... | collective-permute-start | bytes 7962632 | tf_op jit(solution)/shard_map/ppermute | solution.py:319
  278.6 67.3 %collective-permute-start.22 = (bf16[1152,1152]{1,0:T(8,128)(2,1)}, bf16[1152,1152]{1,0:T(8,128)(2,1)}, u32[]{:S(2)}, u32[]{:S(2)}) collective-permute-start(bf16[1152,1152]{1,0:T(8,128)(2,1)} %collective-permute-done.21.b0), channel_id=1, source_target_pairs={{0,1},{1,0},{2,3},{3,2},{4,5},{5,4},{6,7},{7,6},{8,9},{9,8},{10,11... | collective-permute-start | bytes 7962632 | tf_op jit(solution)/shard_map/ppermute | solution.py:319
  337.1 64.2 %collective-permute-start.39 = (bf16[1152,1152]{1,0:T(8,128)(2,1)}, bf16[1152,1152]{1,0:T(8,128)(2,1)}, u32[]{:S(2)}, u32[]{:S(2)}) collective-permute-start(bf16[1152,1152]{1,0:T(8,128)(2,1)} %get-tuple-element.92), channel_id=1, source_target_pairs={{0,1},{1,0},{2,3},{3,2},{4,5},{5,4},{6,7},{7,6},{8,9},{9,8},{10,11... | collective-permute-start | bytes 7962632 | tf_op jit(solution)/shard_map/ppermute | solution.py:319
  345.7 60.3 %collective-permute-start.19 = (bf16[1152,1152]{1,0:T(8,128)(2,1)}, bf16[1152,1152]{1,0:T(8,128)(2,1)}, u32[]{:S(2)}, u32[]{:S(2)}) collective-permute-start(bf16[1152,1152]{1,0:T(8,128)(2,1)} %collective-permute-done.18.b0), channel_id=1, source_target_pairs={{0,1},{1,0},{2,3},{3,2},{4,5},{5,4},{6,7},{7,6},{8,9},{9,8},{10,11... | collective-permute-start | bytes 7962632 | tf_op jit(solution)/shard_map/ppermute | solution.py:319
  399.5 137.0 %collective-permute-start.40 = (bf16[1152,1152]{1,0:T(8,128)(2,1)}, bf16[1152,1152]{1,0:T(8,128)(2,1)}, u32[]{:S(2)}, u32[]{:S(2)}) collective-permute-start(bf16[1152,1152]{1,0:T(8,128)(2,1)} %get-tuple-element.94), channel_id=1, source_target_pairs={{0,1},{1,0},{2,3},{3,2},{4,5},{5,4},{6,7},{7,6},{8,9},{9,8},{10,11... | collective-permute-start | bytes 7962632 | tf_op jit(solution)/shard_map/ppermute | solution.py:319
  399.8 33.1 %collective-permute-start.42 = (bf16[1152,1152]{1,0:T(8,128)(2,1)}, bf16[1152,1152]{1,0:T(8,128)(2,1)}, u32[]{:S(2)}, u32[]{:S(2)}) collective-permute-start(bf16[1152,1152]{1,0:T(8,128)(2,1)} %get-tuple-element.96), channel_id=1, source_target_pairs={{0,1},{1,0},{2,3},{3,2},{4,5},{5,4},{6,7},{7,6},{8,9},{9,8},{10,11... | collective-permute-start | bytes 7962632 | tf_op jit(solution)/shard_map/ppermute | solution.py:319
  432.6 154.8 %collective-permute-start.43 = (bf16[1152,1152]{1,0:T(8,128)(2,1)}, bf16[1152,1152]{1,0:T(8,128)(2,1)}, u32[]{:S(2)}, u32[]{:S(2)}) collective-permute-start(bf16[1152,1152]{1,0:T(8,128)(2,1)} %get-tuple-element.98), channel_id=1, source_target_pairs={{0,1},{1,0},{2,3},{3,2},{4,5},{5,4},{6,7},{7,6},{8,9},{9,8},{10,11... | collective-permute-start | bytes 7962632 | tf_op jit(solution)/shard_map/ppermute | solution.py:319
  479.6 74.7 %collective-permute-start.31 = (bf16[576,1152]{1,0:T(8,128)(2,1)}, bf16[576,1152]{1,0:T(8,128)(2,1)}, u32[]{:S(2)}, u32[]{:S(2)}) collective-permute-start(bf16[576,1152]{1,0:T(8,128)(2,1)} %get-tuple-element.86), channel_id=1, source_target_pairs={{0,1},{1,0},{2,3},{3,2},{4,5},{5,4},{6,7},{7,6},{8,9},{9,8},{10,11... | collective-permute-start | bytes 3981320 | tf_op jit(solution)/shard_map/ppermute | solution.py:319
  479.8 68.4 %collective-permute-start.34 = (bf16[576,1152]{1,0:T(8,128)(2,1)}, bf16[576,1152]{1,0:T(8,128)(2,1)}, u32[]{:S(2)}, u32[]{:S(2)}) collective-permute-start(bf16[576,1152]{1,0:T(8,128)(2,1)} %get-tuple-element.90), channel_id=1, source_target_pairs={{0,1},{1,0},{2,3},{3,2},{4,5},{5,4},{6,7},{7,6},{8,9},{9,8},{10,11... | collective-permute-start | bytes 3981320 | tf_op jit(solution)/shard_map/ppermute | solution.py:319
  498.9 58.6 %collective-permute-start.33 = (bf16[576,1152]{1,0:T(8,128)(2,1)}, bf16[576,1152]{1,0:T(8,128)(2,1)}, u32[]{:S(2)}, u32[]{:S(2)}) collective-permute-start(bf16[576,1152]{1,0:T(8,128)(2,1)} %get-tuple-element.88), channel_id=1, source_target_pairs={{0,1},{1,0},{2,3},{3,2},{4,5},{5,4},{6,7},{7,6},{8,9},{9,8},{10,11... | collective-permute-start | bytes 3981320 | tf_op jit(solution)/shard_map/ppermute | solution.py:319
  541.5 43.0 %collective-permute-start.24 = (bf16[4,320,1152]{2,1,0:T(8,128)(2,1)S(1)}, bf16[4,320,1152]{2,1,0:T(8,128)(2,1)S(1)}, u32[]{:S(2)}, u32[]{:S(2)}) collective-permute-start(bf16[4,320,1152]{2,1,0:T(8,128)(2,1)S(1)} %pad_maximum_fusion.1), channel_id=1, source_target_pairs={{0,1},{1,0},{2,3},{3,2},{4,5},{5,4},{6,7},{7,6},{8,9},{9,8},{10,11... | collective-permute-start | bytes 8847368 | tf_op jit(solution)/shard_map/ppermute | solution.py:319
  550.1 32.1 %collective-permute-start.35 = (bf16[576,1152]{1,0:T(8,128)(2,1)S(1)}, bf16[576,1152]{1,0:T(8,128)(2,1)S(1)}, u32[]{:S(2)}, u32[]{:S(2)}) collective-permute-start(bf16[576,1152]{1,0:T(8,128)(2,1)S(1)} %add_convert_fusion.16), channel_id=1, source_target_pairs={{0,4},{1,5},{2,6},{3,7},{4,0},{5,1},{6,2},{7,3},{8,12},{9,13},{10,... | collective-permute-start | bytes 3981320 | tf_op jit(solution)/shard_map/ppermute | solution.py:319
  554.3 208.4 %collective-permute-start.41 = (bf16[576,1152]{1,0:T(8,128)(2,1)}, bf16[576,1152]{1,0:T(8,128)(2,1)}, u32[]{:S(2)}, u32[]{:S(2)}) collective-permute-start(bf16[576,1152]{1,0:T(8,128)(2,1)} %slice.430), channel_id=1, source_target_pairs={{0,4},{1,5},{2,6},{3,7},{4,0},{5,1},{6,2},{7,3},{8,12},{9,13},{10,... | collective-permute-start | bytes 3981320 | tf_op jit(solution)/shard_map/ppermute | solution.py:319
  557.5 99.3 %collective-permute-start.30 = (bf16[576,1152]{1,0:T(8,128)(2,1)S(1)}, bf16[576,1152]{1,0:T(8,128)(2,1)S(1)}, u32[]{:S(2)}, u32[]{:S(2)}) collective-permute-start(bf16[576,1152]{1,0:T(8,128)(2,1)S(1)} %copy-done.34), channel_id=1, source_target_pairs={{0,1},{1,0},{2,3},{3,2},{4,5},{5,4},{6,7},{7,6},{8,9},{9,8},{10,11... | collective-permute-start | bytes 3981320 | tf_op jit(solution)/shard_map/ppermute | solution.py:319
  582.2 75.1 %collective-permute-start.32 = (bf16[576,1152]{1,0:T(8,128)(2,1)S(1)}, bf16[576,1152]{1,0:T(8,128)(2,1)S(1)}, u32[]{:S(2)}, u32[]{:S(2)}) collective-permute-start(bf16[576,1152]{1,0:T(8,128)(2,1)S(1)} %add_convert_fusion.19), channel_id=1, source_target_pairs={{0,4},{1,5},{2,6},{3,7},{4,0},{5,1},{6,2},{7,3},{8,12},{9,13},{10,... | collective-permute-start | bytes 3981320 | tf_op jit(solution)/shard_map/ppermute | solution.py:319
  584.5 73.3 %collective-permute-start.36 = (bf16[576,1152]{1,0:T(8,128)(2,1)S(1)}, bf16[576,1152]{1,0:T(8,128)(2,1)S(1)}, u32[]{:S(2)}, u32[]{:S(2)}) collective-permute-start(bf16[576,1152]{1,0:T(8,128)(2,1)S(1)} %add_convert_fusion.15), channel_id=1, source_target_pairs={{0,2},{1,3},{2,0},{3,1},{4,6},{5,7},{6,4},{7,5},{8,10},{9,11},{10,... | collective-permute-start | bytes 3981320 | tf_op jit(solution)/shard_map/ppermute | solution.py:319
  587.5 66.6 %collective-permute-start.26 = (bf16[320,1152]{1,0:T(8,128)(2,1)S(1)}, bf16[320,1152]{1,0:T(8,128)(2,1)S(1)}, u32[]{:S(2)}, u32[]{:S(2)}) collective-permute-start(bf16[320,1152]{1,0:T(8,128)(2,1)S(1)} %get-tuple-element.168), channel_id=1, source_target_pairs={{0,4},{1,5},{2,6},{3,7},{4,0},{5,1},{6,2},{7,3},{8,12},{9,13},{10,... | collective-permute-start | bytes 2211848 | tf_op jit(solution)/shard_map/ppermute | solution.py:319
  654.1 32.0 %collective-permute-start.47 = (bf16[576,1152]{1,0:T(8,128)(2,1)S(1)}, bf16[576,1152]{1,0:T(8,128)(2,1)S(1)}, u32[]{:S(2)}, u32[]{:S(2)}) collective-permute-start(bf16[576,1152]{1,0:T(8,128)(2,1)S(1)} %get-tuple-element.178), channel_id=1, source_target_pairs={{0,2},{1,3},{2,0},{3,1},{4,6},{5,7},{6,4},{7,5},{8,10},{9,11},{10,... | collective-permute-start | bytes 3981320 | tf_op jit(solution)/shard_map/ppermute | solution.py:319
  656.9 107.6 %collective-permute-start.46 = (bf16[576,1152]{1,0:T(8,128)(2,1)}, bf16[576,1152]{1,0:T(8,128)(2,1)}, u32[]{:S(2)}, u32[]{:S(2)}) collective-permute-start(bf16[576,1152]{1,0:T(8,128)(2,1)} %slice.434), channel_id=1, source_target_pairs={{0,2},{1,3},{2,0},{3,1},{4,6},{5,7},{6,4},{7,5},{8,10},{9,11},{10,... | collective-permute-start | bytes 3981320 | tf_op jit(solution)/shard_map/ppermute | solution.py:319
  657.3 34.6 %collective-permute-start.44 = (bf16[576,1152]{1,0:T(8,128)(2,1)}, bf16[576,1152]{1,0:T(8,128)(2,1)}, u32[]{:S(2)}, u32[]{:S(2)}) collective-permute-start(bf16[576,1152]{1,0:T(8,128)(2,1)} %get-tuple-element.177), channel_id=1, source_target_pairs={{0,4},{1,5},{2,6},{3,7},{4,0},{5,1},{6,2},{7,3},{8,12},{9,13},{10,... | collective-permute-start | bytes 3981320 | tf_op jit(solution)/shard_map/ppermute | solution.py:319
  657.8 47.6 %collective-permute-start.25 = (bf16[320,1152]{1,0:T(8,128)(2,1)}, bf16[320,1152]{1,0:T(8,128)(2,1)}, u32[]{:S(2)}, u32[]{:S(2)}) collective-permute-start(bf16[320,1152]{1,0:T(8,128)(2,1)} %get-tuple-element.167), channel_id=1, source_target_pairs={{0,4},{1,5},{2,6},{3,7},{4,0},{5,1},{6,2},{7,3},{8,12},{9,13},{10,... | collective-permute-start | bytes 2211848 | tf_op jit(solution)/shard_map/ppermute | solution.py:319
  686.1 44.3 %collective-permute-start.27 = (bf16[320,1152]{1,0:T(8,128)(2,1)}, bf16[320,1152]{1,0:T(8,128)(2,1)}, u32[]{:S(2)}, u32[]{:S(2)}) collective-permute-start(bf16[320,1152]{1,0:T(8,128)(2,1)} %add_convert_fusion.23), channel_id=1, source_target_pairs={{0,2},{1,3},{2,0},{3,1},{4,6},{5,7},{6,4},{7,5},{8,10},{9,11},{10,... | collective-permute-start | bytes 2211848 | tf_op jit(solution)/shard_map/ppermute | solution.py:319
  692.0 72.5 %collective-permute-start.48 = (bf16[576,1152]{1,0:T(8,128)(2,1)}, bf16[576,1152]{1,0:T(8,128)(2,1)S(1)}, u32[]{:S(2)}, u32[]{:S(2)}) collective-permute-start(bf16[576,1152]{1,0:T(8,128)(2,1)} %add_convert_fusion.9), channel_id=1, source_target_pairs={{0,4},{1,5},{2,6},{3,7},{4,0},{5,1},{6,2},{7,3},{8,12},{9,13},{10,... | collective-permute-start | bytes 3981320 | tf_op jit(solution)/shard_map/ppermute | solution.py:319
  705.4 59.1 %collective-permute-start.45 = (bf16[576,1152]{1,0:T(8,128)(2,1)S(1)}, bf16[576,1152]{1,0:T(8,128)(2,1)S(1)}, u32[]{:S(2)}, u32[]{:S(2)}) collective-permute-start(bf16[576,1152]{1,0:T(8,128)(2,1)S(1)} %add_convert_fusion.12), channel_id=1, source_target_pairs={{0,2},{1,3},{2,0},{3,1},{4,6},{5,7},{6,4},{7,5},{8,10},{9,11},{10,... | collective-permute-start | bytes 3981320 | tf_op jit(solution)/shard_map/ppermute | solution.py:319
  730.4 31.9 %collective-permute-start.37 = (bf16[2,288,576]{2,1,0:T(8,128)(2,1)S(1)}, bf16[2,288,576]{2,1,0:T(8,128)(2,1)S(1)}, u32[]{:S(2)}, u32[]{:S(2)}) collective-permute-start(bf16[2,288,576]{2,1,0:T(8,128)(2,1)S(1)} %constant_dynamic-slice_fusion.3), channel_id=1, source_target_pairs={{0,16},{8,24},{16,0},{24,8},{1,17},{9,25},{17,1},{25,9},{2,18},{10... | collective-permute-start | bytes 1990664 | tf_op jit(solution)/shard_map/ppermute | solution.py:378
  762.4 18.8 %collective-permute-start.28 = (bf16[2,80,1152]{2,1,0:T(8,128)(2,1)S(1)}, bf16[2,80,1152]{2,1,0:T(8,128)(2,1)}, u32[]{:S(2)}, u32[]{:S(2)}) collective-permute-start(bf16[2,80,1152]{2,1,0:T(8,128)(2,1)S(1)} %constant_dynamic-slice_fusion.5), channel_id=1, source_target_pairs={{0,16},{8,24},{16,0},{24,8},{1,17},{9,25},{17,1},{25,9},{2,18},{10... | collective-permute-start | bytes 1105928 | tf_op jit(solution)/shard_map/ppermute | solution.py:378
  762.7 20.4 %collective-permute-start.38 = (bf16[1,288,576]{2,1,0:T(8,128)(2,1)S(1)}, bf16[1,288,576]{2,1,0:T(8,128)(2,1)}, u32[]{:S(2)}, u32[]{:S(2)}) collective-permute-start(bf16[1,288,576]{2,1,0:T(8,128)(2,1)S(1)} %constant_dynamic-slice_fusion.2), channel_id=1, source_target_pairs={{0,8},{8,0},{16,24},{24,16},{1,9},{9,1},{17,25},{25,17},{2,10},{10... | collective-permute-start | bytes 995336 | tf_op jit(solution)/shard_map/ppermute | solution.py:378
  774.3 63.0 %collective-permute-start.49 = (bf16[2,288,1152]{2,1,0:T(8,128)(2,1)}, bf16[2,288,1152]{2,1,0:T(8,128)(2,1)}, u32[]{:S(2)}, u32[]{:S(2)}) collective-permute-start(bf16[2,288,1152]{2,1,0:T(8,128)(2,1)} %constant_dynamic-slice_fusion.1), channel_id=1, source_target_pairs={{0,16},{8,24},{16,0},{24,8},{1,17},{9,25},{17,1},{25,9},{2,18},{10... | collective-permute-start | bytes 3981320 | tf_op jit(solution)/shard_map/ppermute | solution.py:378
  783.0 28.2 %collective-permute-start.29 = (bf16[1,80,1152]{2,1,0:T(8,128)(2,1)}, bf16[1,80,1152]{2,1,0:T(8,128)(2,1)}, u32[]{:S(2)}, u32[]{:S(2)}) collective-permute-start(bf16[1,80,1152]{2,1,0:T(8,128)(2,1)} %constant_dynamic-slice_fusion.4), channel_id=1, source_target_pairs={{0,8},{8,0},{16,24},{24,16},{1,9},{9,1},{17,25},{25,17},{2,10},{10... | collective-permute-start | bytes 552968 | tf_op jit(solution)/shard_map/ppermute | solution.py:378
  (39 other events, 603.4 us)
